TPU v7x, 256 devices: a 4x2x16 block of a 4x16x16 slice. The times are simulated.
256 devices in a mesh: groups: 2 (over y), ctx: 128 (over z, x, core).
Axes of the slice: x: 4, y: 2, z: 16, core: 2. Of those that a mesh axis runs over, the one named last changes fastest.
The devices are a block of a 4x16x16 slice.
Arguments:
- queries: bfloat16 [512, 5120], P('groups'), parts along dimension 0, may hold values from -400 to 400
- new_keys: bfloat16 [512, 5120], P(('groups', 'ctx')), parts along dimension 0, may hold values from -15 to 15
- new_values: bfloat16 [512, 5120], P(('groups', 'ctx')), parts along dimension 0, may hold values from -6 to 6
- cache_keys: bfloat16 [8, 256, 32, 5120], P('groups', 'ctx'), parts along dimension 0, may hold values from -5 to 5
- cache_values: bfloat16 [8, 256, 32, 5120], P('groups', 'ctx'), parts along dimension 0, may hold values from -6 to 6
- slot_of: int32 [8], P('groups'), parts along dimension 0, may hold values from 0 to 3, as said below
- cached: int32 [8], P('groups'), parts along dimension 0, may hold values from 1 to 256, as said below
- actions: int32 [8, 8], P('groups'), parts along dimension 0, may hold values from 0 to 255
- action_table: bfloat16 [256, 5120], replicated, may hold values from -3 to 3
- null_gate: float32 [5120], replicated, may hold values from -3 to 3
- residual: bfloat16 [512, 5120], P(('groups', 'ctx')), parts along dimension 0, may hold values from -3 to 3
- out_weight: bfloat16 [5120, 5120], P('ctx'), may hold values from -0.078125 to 0.078125
Outputs:
- branch_out: bfloat16 [512, 5120], P(('groups', 'ctx')), parts along dimension 0
There are 2 independent parts, one for each index of `groups`. A program takes and returns all parts, laid end to end along the dimension named above; an argument that names none is the same for every part. Nothing has to cross between parts.
Inputs may be any that keep to these rules, and one draw needn't show every extreme that they name: `slot_of`: the 4 sessions have different slots. Some session has all 256 frames cached.
All inputs are finite; a program needn't handle non-finite values.
Results may differ from a plain program's by a relative error of at most 0.0042.
Values may be sent and summed in bfloat16 or wider, within the bound.
A program may use at most 128 MiB of HBM per device.

v0:
```python
import math

import jax
import jax.numpy as jnp
from jax import lax
from jax.sharding import Mesh
from jax.sharding import PartitionSpec as P

HEADS = 40
NEWTOK = 32
CTX = ("ctx_0", "ctx_1", "ctx_2")
GROUPS_CTX = ("groups", "ctx_0", "ctx_1", "ctx_2")


masked_score = -1e30


def sent_to_all(value, axis):
    length = lax.axis_size(axis)
    return lax.all_to_all(
        jnp.broadcast_to(value[None], (length, *value.shape)), axis, 0, 0, tiled=True
    )


def taken_together(value, axis):
    everything = sent_to_all(value, axis)
    return jnp.max(everything, axis=0)


def by_axis(value, axes):
    far, near = axes
    return taken_together(taken_together(value, near), far)


def split_up(value, dim, length):
    shape = value.shape
    blocks = value.reshape(*shape[:dim], length, shape[dim] // length, *shape[dim + 1 :])
    return jnp.moveaxis(blocks, dim, 0)


def summed_on_arrival(value, axis, dim):
    length = lax.axis_size(axis)
    blocks = lax.all_to_all(split_up(value, dim, length), axis, 0, 0, tiled=True)
    return jnp.sum(blocks, axis=0)


def sum_in_two_steps(value, axes, dim):
    far, near = axes
    blocks = split_up(value, dim, lax.axis_size(far))
    nearer = summed_on_arrival(blocks, near, dim + 1)
    arrived = lax.all_to_all(nearer, far, split_axis=0, concat_axis=0, tiled=True)
    return arrived.sum(axis=0)


def padded_to(lines, length):
    spare = -lines.shape[0] % length
    if not spare:
        return lines
    return jnp.concatenate([lines, jnp.zeros((spare, *lines.shape[1:]), lines.dtype)])


def laid_out(blocks, dim):
    shape = list(blocks.shape[1:])
    shape[dim] *= blocks.shape[0]
    return jnp.moveaxis(blocks, 0, dim).reshape(shape)


def gathered_by_axis(value, axes, dim):
    far, near = axes
    first = sent_to_all(value, far)
    blocks = jnp.swapaxes(sent_to_all(first, near), 0, 1)
    return laid_out(blocks.reshape(-1, *value.shape), dim)


def sum_by_parts(value, axes):
    lines = value.reshape(-1, value.shape[-1])
    own = sum_in_two_steps(
        padded_to(lines, lax.axis_size(axes[0]) * lax.axis_size(axes[1])), axes, 0
    )
    whole = gathered_by_axis(own, axes, 0)
    return whole[: len(lines)].reshape(value.shape)


def on_device(
    queries,
    new_keys,
    new_values,
    cache_keys,
    cache_values,
    slot_of,
    cached,
    actions,
    action_table,
    null_gate,
    residual,
    out_weight,
):
    total_rows, model_dim = queries.shape
    head_dim = model_dim // HEADS
    scaling = 1.0 / math.sqrt(head_dim)
    sessions = slot_of.shape[0]
    session_rows = total_rows // sessions
    frames_here = cache_keys.shape[1]
    local_keys = frames_here * NEWTOK
    devices = lax.axis_size(CTX)
    position = lax.axis_index(CTX)
    own_rows = new_keys.shape[0]
    grouped = queries.reshape(sessions, session_rows, HEADS, head_dim)
    slot_keys = jnp.take(cache_keys, slot_of, axis=0).reshape(sessions, local_keys, HEADS, head_dim)
    slot_values = jnp.take(cache_values, slot_of, axis=0).reshape(
        sessions, local_keys, HEADS, head_dim
    )
    cache_scores = (
        jnp.einsum("sqhd,skhd->shqk", grouped, slot_keys, preferred_element_type=jnp.float32)
        * scaling
    )
    frame_ids = position * frames_here + jnp.arange(local_keys) // NEWTOK
    live_keys = frame_ids[None, :] < cached[:, None]
    cache_scores = jnp.where(live_keys[:, None, None, :], cache_scores, masked_score)
    query_ids = jnp.arange(total_rows)
    key_ids = position * own_rows + jnp.arange(own_rows)
    same_session = query_ids[:, None] // session_rows == key_ids[None, :] // session_rows
    same_branch = query_ids[:, None] % 2 == key_ids[None, :] % 2
    own_scores = (
        jnp.einsum(
            "qhd,khd->hqk",
            queries.reshape(total_rows, HEADS, head_dim),
            new_keys.reshape(own_rows, HEADS, head_dim),
            preferred_element_type=jnp.float32,
        )
        * scaling
    )
    own_scores = jnp.where((same_session & same_branch)[None], own_scores, masked_score)
    cache_top = cache_scores.max(-1).transpose(0, 2, 1).reshape(total_rows, HEADS)
    local_top = jnp.maximum(cache_top, own_scores.max(-1).T)
    highest = by_axis(local_top, ("ctx_0", ("ctx_1", "ctx_2")))
    session_top = highest.reshape(sessions, session_rows, HEADS).transpose(0, 2, 1)
    cache_weights = jnp.exp(cache_scores - session_top[..., None])
    own_weights = jnp.exp(own_scores - highest.T[..., None])
    partial_totals = (
        cache_weights.sum(-1).transpose(0, 2, 1).reshape(total_rows, HEADS) + own_weights.sum(-1).T
    )
    cache_numer = jnp.einsum(
        "shqk,skhd->sqhd",
        cache_weights.astype(jnp.bfloat16),
        slot_values,
        preferred_element_type=jnp.float32,
    ).reshape(total_rows, model_dim)
    own_numer = jnp.einsum(
        "hqk,khd->qhd",
        own_weights.astype(jnp.bfloat16),
        new_values.reshape(own_rows, HEADS, head_dim),
        preferred_element_type=jnp.float32,
    ).reshape(total_rows, model_dim)
    numer_share = sum_in_two_steps(cache_numer + own_numer, (("ctx_0", "ctx_1"), "ctx_2"), 1)
    totals = sum_by_parts(partial_totals, (("ctx_0", "ctx_1"), "ctx_2"))
    share_dim = model_dim // devices
    feature_heads = (position * share_dim + jnp.arange(share_dim)) // head_dim
    totals_here = jnp.take(totals, feature_heads, axis=1)
    attended = (numer_share / totals_here).astype(jnp.bfloat16)
    vocab_size = action_table.shape[0]
    action_counts = (
        (actions[:, :, None] == jnp.arange(vocab_size, dtype=jnp.int32)[None, None, :])
        .astype(jnp.float32)
        .sum(1)
    )
    cond_gate = (
        1.0
        + jnp.dot(
            action_counts.astype(jnp.bfloat16), action_table, preferred_element_type=jnp.float32
        )
        / actions.shape[1]
    )
    uncond_gate = 1.0 + null_gate
    rows_here = residual.shape[0]
    projected = sum_in_two_steps(
        jnp.dot(attended, out_weight, preferred_element_type=jnp.float32),
        (("ctx_0", "ctx_1"), "ctx_2"),
        0,
    )
    row_ids = position * rows_here + jnp.arange(rows_here)
    cond_rows = jnp.take(cond_gate, row_ids // session_rows, axis=0)
    gate_rows = jnp.where((row_ids % 2 == 0)[:, None], cond_rows, uncond_gate[None, :])
    return (residual.astype(jnp.float32) + gate_rows * projected).astype(jnp.bfloat16)


def solution(mesh):
    split = Mesh(
        mesh.devices.reshape(mesh.shape["groups"], 16, 4, 2), ("groups", "ctx_0", "ctx_1", "ctx_2")
    )
    in_specs = (
        P("groups", None),
        P(GROUPS_CTX, None),
        P(GROUPS_CTX, None),
        P("groups", CTX, None, None),
        P("groups", CTX, None, None),
        P("groups"),
        P("groups"),
        P("groups", None),
        P(),
        P(),
        P(GROUPS_CTX, None),
        P(CTX, None),
    )
    out_specs = P(GROUPS_CTX, None)
    return jax.shard_map(
        on_device, mesh=split, in_specs=in_specs, out_specs=out_specs, check_vma=False
    )
```

profile of v0, /device:TPU:33, one launch (start us, length us, event | category | flops | bytes accessed | tf_op | source)
XLA Modules:
  0.0 503.6 jit_solution(4966064023393421607)
XLA Ops:
  4.0 4.0 gather_fusion.3
  7.9 4.6 broadcast_select_fusion.1
  15.0 3.8 bitcast_reduce_fusion
  19.9 30.3 %all_to_all.50 = f32[8,256,40]{1,2,0:T(8,128)S(1)} all-to-all(f32[8,256,40]{1,2,0:T(8,128)S(1)} %broadcast_in_dim.115), channel_id=1, replica_groups=mesh['groups'=2,'ctx_0'=16,'ctx_1'=4,'ctx_2'=2] {'ctx_1','ctx_2'}, dimensions={0} | all-to-all | bytes 655360 | tf_op jit(solution)/shard_map/all_to_all | solution.py:20
  51.2 6.6 %all-to-all-start.1 = ((f32[16,256,40]{1,2,0:T(8,128)}), f32[16,256,40]{1,2,0:T(8,128)S(1)}, u32[]{:S(2)}, u32[]{:S(2)}) async-start(f32[16,256,40]{1,2,0:T(8,128)} %broadcast_in_dim.116), calls=%async_computation.1 | async-start | bytes 1310720 | tf_op jit(solution)/shard_map/all_to_all | solution.py:20
  60.1 26.4 %all-to-all-done.1 = f32[16,256,40]{1,2,0:T(8,128)S(1)} async-done(((f32[16,256,40]{1,2,0:T(8,128)}), f32[16,256,40]{1,2,0:T(8,128)S(1)}, u32[]{:S(2)}, u32[]{:S(2)}) %all-to-all-start.1) | async-done | bytes 655392 | tf_op jit(solution)/shard_map/all_to_all | solution.py:20
  86.7 4.1 fusion.2
  91.4 9.1 %all_to_all.51 = f32[2,1,5120]{2,1,0:T(1,128)S(1)} all-to-all(f32[2,1,5120]{2,1,0:T(1,128)S(1)} %reshape.448), channel_id=1, replica_groups=mesh['groups'=2,'ctx_0'=16,'ctx_1'=4,'ctx_2'=2] {'ctx_2'}, dimensions={0} | all-to-all | bytes 81920 | tf_op jit(solution)/shard_map/all_to_all | solution.py:43
  102.7 10.4 %all-to-all-start.5 = ((f32[64,2,40]{2,1,0:T(2,128)}), f32[64,2,40]{2,1,0:T(2,128)S(1)}, u32[]{:S(2)}, u32[]{:S(2)}) async-start(f32[64,2,40]{2,1,0:T(2,128)} %copy.148), calls=%async_computation.5 | async-start | bytes 131072 | tf_op jit(solution)/shard_map/all_to_all | solution.py:51
  113.1 4.1 fusion.17
  117.1 5.4 %copy.139 = f32[4,64,40,128]{3,2,1,0:T(8,128)} copy(f32[4,64,40,128]{3,1,2,0:T(8,128)S(1)} %fusion.17) | data formatting | bytes 10485760 | tf_op jit(solution)/shard_map/shqk,skhd->sqhd/transpose | solution.py:143
  122.6 8.8 %reshape.405 = f32[256,64,80]{2,1,0:T(8,128)} reshape(f32[4,64,40,128]{3,2,1,0:T(8,128)} %copy.139) | data formatting | bytes 10485760 | tf_op jit(solution)/shard_map/reshape | solution.py:148
  131.3 3.2 fusion.30
  134.5 7.9 %copy.141 = f32[256,64,80]{2,1,0:T(8,128)} copy(f32[256,64,80]{0,2,1:T(8,128)} %bitcast.100) | data formatting | bytes 10485760 | tf_op jit(solution)/shard_map/reshape | solution.py:154
  142.5 12.0 %add_bitcast_fusion = f32[64,256,80]{2,0,1:T(8,128)} fusion(f32[256,64,80]{2,1,0:T(8,128)} %reshape.405, f32[256,64,80]{2,1,0:T(8,128)} %copy.141), kind=kLoop, calls=%fused_computation.4 | loop fusion | flops 1310720 | bytes 15728640 | tf_op jit(solution)/shard_map/transpose | solution.py:38
  154.5 8.3 %copy.142 = f32[64,256,80]{1,2,0:T(8,128)} copy(f32[64,256,80]{2,0,1:T(8,128)} %add_bitcast_fusion) | data formatting | bytes 10485760 | tf_op jit(solution)/shard_map/transpose | solution.py:38
  162.8 5.3 %copy.143 = f32[2,64,256,40]{2,3,1,0:T(8,128)} copy(f32[2,64,256,40]{2,3,0,1:T(8,128)} %bitcast.101) | data formatting | bytes 10485760 | tf_op jit(solution)/shard_map/transpose | solution.py:38
  168.0 6.6 %all-to-all-start.2 = ((f32[2,64,256,40]{2,3,1,0:T(8,128)}), f32[2,64,256,40]{2,3,1,0:T(8,128)}, u32[]{:S(2)}, u32[]{:S(2)}) async-start(f32[2,64,256,40]{2,3,1,0:T(8,128)} %copy.143), calls=%async_computation.2 | async-start | bytes 10485760 | tf_op jit(solution)/shard_map/all_to_all | solution.py:43
  174.7 4.8 all-to-all-done.2
  180.1 15.8 %all-to-all-start.6 = ((f32[64,2,40]{2,1,0:T(2,128)}), f32[64,2,40]{2,1,0:T(2,128)S(1)}, u32[]{:S(2)}, u32[]{:S(2)}) async-start(f32[64,2,40]{2,1,0:T(2,128)} %broadcast_in_dim.118), calls=%async_computation.6 | async-start | bytes 131072 | tf_op jit(solution)/shard_map/all_to_all | solution.py:20
  196.0 4.7 reduce_sum.82
  200.6 7.8 %all-to-all-done.6 = f32[64,2,40]{2,1,0:T(2,128)S(1)} async-done(((f32[64,2,40]{2,1,0:T(2,128)}), f32[64,2,40]{2,1,0:T(2,128)S(1)}, u32[]{:S(2)}, u32[]{:S(2)}) %all-to-all-start.6) | async-done | bytes 20512 | tf_op jit(solution)/shard_map/all_to_all | solution.py:20
  208.6 5.7 %all_to_all.52 = f32[2,1,5120]{2,1,0:T(1,128)S(1)} all-to-all(f32[2,1,5120]{2,1,0:T(1,128)S(1)} %reshape.450), channel_id=1, replica_groups=mesh['groups'=2,'ctx_0'=16,'ctx_1'=4,'ctx_2'=2] {'ctx_2'}, dimensions={0} | all-to-all | bytes 81920 | tf_op jit(solution)/shard_map/all_to_all | solution.py:20
  214.3 7.2 %all-to-all-start.3 = ((f32[64,256,40]{1,2,0:T(8,128)}), f32[64,256,40]{1,2,0:T(8,128)}, u32[]{:S(2)}, u32[]{:S(2)}) async-start(f32[64,256,40]{1,2,0:T(8,128)} %reduce_sum.82), calls=%async_computation.3 | async-start | bytes 5242880 | tf_op jit(solution)/shard_map/all_to_all | solution.py:51
  223.4 115.8 %all-to-all-done.3 = f32[64,256,40]{1,2,0:T(8,128)} async-done(((f32[64,256,40]{1,2,0:T(8,128)}), f32[64,256,40]{1,2,0:T(8,128)}, u32[]{:S(2)}, u32[]{:S(2)}) %all-to-all-start.3) | async-done | bytes 2621472 | tf_op jit(solution)/shard_map/all_to_all | solution.py:51
  341.0 3.3 fusion.34
  344.3 7.2 %reshape_reshape.11 = f32[64,2,2,5120]{3,2,1,0:T(2,128)} reshape(f32[256,5120]{1,0:T(8,128)} %fusion.34) | data formatting | bytes 10485760 | tf_op jit(solution)/shard_map/reshape;reshape | solution.py:37
  351.5 2.9 copy.184
  354.4 13.4 %all_to_all.53 = f32[2,64,2,5120]{3,2,1,0:T(2,128)} all-to-all(f32[2,64,2,5120]{3,2,1,0:T(2,128)S(1)} %bitcast.102), channel_id=1, replica_groups=mesh['groups'=2,'ctx_0'=16,'ctx_1'=4,'ctx_2'=2] {'ctx_2'}, dimensions={0} | all-to-all | bytes 10485760 | tf_op jit(solution)/shard_map/all_to_all | solution.py:43
  367.8 7.8 %reduce_sum.88 = f32[64,2,5120]{2,1,0:T(2,128)} reduce(f32[2,64,2,5120]{3,2,1,0:T(2,128)} %all_to_all.53, f32[]{:T(128)} %constant.152.clone.1), dimensions={0}, to_apply=%region_11.13 | reduce | flops 655360 | bytes 7864324 | tf_op jit(solution)/shard_map/reduce_sum | solution.py:44
  375.6 7.4 %all-to-all-start.9 = ((f32[64,2,5120]{2,1,0:T(2,128)}), f32[64,2,5120]{2,1,0:T(2,128)}, u32[]{:S(2)}, u32[]{:S(2)}) async-start(f32[64,2,5120]{2,1,0:T(2,128)} %reduce_sum.88), calls=%async_computation.9 | async-start | bytes 5242880 | tf_op jit(solution)/shard_map/all_to_all | solution.py:51
  386.1 114.4 %all-to-all-done.9 = f32[64,2,5120]{2,1,0:T(2,128)} async-done(((f32[64,2,5120]{2,1,0:T(2,128)}), f32[64,2,5120]{2,1,0:T(2,128)}, u32[]{:S(2)}, u32[]{:S(2)}) %all-to-all-start.9) | async-done | bytes 2621472 | tf_op jit(solution)/shard_map/all_to_all | solution.py:51
  (81 shorter events, 24.4 us)
Async XLA Ops:
  0.0 1.8 copy-start
  12.5 1.7 copy-start.2
  14.2 0.7 copy-start.10
  15.0 4.0 copy-start.3
  15.0 4.0 copy-start.9
  51.2 35.3 %all-to-all-start.1 = ((f32[16,256,40]{1,2,0:T(8,128)}), f32[16,256,40]{1,2,0:T(8,128)S(1)}, u32[]{:S(2)}, u32[]{:S(2)}) async-start(f32[16,256,40]{1,2,0:T(8,128)} %broadcast_in_dim.116), calls=%async_computation.1 | async-start | bytes 1310720 | tf_op jit(solution)/shard_map/all_to_all | solution.py:20
  102.7 65.4 %all-to-all-start.5 = ((f32[64,2,40]{2,1,0:T(2,128)}), f32[64,2,40]{2,1,0:T(2,128)S(1)}, u32[]{:S(2)}, u32[]{:S(2)}) async-start(f32[64,2,40]{2,1,0:T(2,128)} %copy.148), calls=%async_computation.5 | async-start | bytes 131072 | tf_op jit(solution)/shard_map/all_to_all | solution.py:51
  122.6 8.8 %copy-start.5 = (bf16[2,5120]{1,0:T(2,128)(2,1)S(1)}, bf16[2,5120]{1,0:T(2,128)(2,1)}, u32[]{:S(2)}) copy-start(bf16[2,5120]{1,0:T(2,128)(2,1)} %param.16) | copy-start | bytes 61444
  168.0 11.5 %all-to-all-start.2 = ((f32[2,64,256,40]{2,3,1,0:T(8,128)}), f32[2,64,256,40]{2,3,1,0:T(8,128)}, u32[]{:S(2)}, u32[]{:S(2)}) async-start(f32[2,64,256,40]{2,3,1,0:T(8,128)} %copy.143), calls=%async_computation.2 | async-start | bytes 10485760 | tf_op jit(solution)/shard_map/all_to_all | solution.py:43
  180.1 28.3 %all-to-all-start.6 = ((f32[64,2,40]{2,1,0:T(2,128)}), f32[64,2,40]{2,1,0:T(2,128)S(1)}, u32[]{:S(2)}, u32[]{:S(2)}) async-start(f32[64,2,40]{2,1,0:T(2,128)} %broadcast_in_dim.118), calls=%async_computation.6 | async-start | bytes 131072 | tf_op jit(solution)/shard_map/all_to_all | solution.py:20
  214.3 124.8 %all-to-all-start.3 = ((f32[64,256,40]{1,2,0:T(8,128)}), f32[64,256,40]{1,2,0:T(8,128)}, u32[]{:S(2)}, u32[]{:S(2)}) async-start(f32[64,256,40]{1,2,0:T(8,128)} %reduce_sum.82), calls=%async_computation.3 | async-start | bytes 5242880 | tf_op jit(solution)/shard_map/all_to_all | solution.py:51
  221.5 119.5 %copy-start.4 = (bf16[40,5120]{1,0:T(8,128)(2,1)S(1)}, bf16[40,5120]{1,0:T(8,128)(2,1)}, u32[]{:S(2)}) copy-start(bf16[40,5120]{1,0:T(8,128)(2,1)} %param.25) | copy-start | bytes 1228804
  375.5 7.4 %copy-start.8 = (s32[4,8]{1,0:T(4,128)S(1)}, s32[4,8]{1,0:T(4,128)}, u32[]{:S(2)}) copy-start(s32[4,8]{1,0:T(4,128)} %param.21) | copy-start | bytes 388
  375.6 124.9 %all-to-all-start.9 = ((f32[64,2,5120]{2,1,0:T(2,128)}), f32[64,2,5120]{2,1,0:T(2,128)}, u32[]{:S(2)}, u32[]{:S(2)}) async-start(f32[64,2,5120]{2,1,0:T(2,128)} %reduce_sum.88), calls=%async_computation.9 | async-start | bytes 5242880 | tf_op jit(solution)/shard_map/all_to_all | solution.py:51
  382.9 3.1 copy-start.7
  383.0 120.7 %copy-start.1 = (bf16[4,2,32,5120]{3,2,1,0:T(8,128)(2,1)S(1)}, bf16[4,2,32,5120]{3,2,1,0:T(8,128)(2,1)}, u32[]{:S(2)}) copy-start(bf16[4,2,32,5120]{3,2,1,0:T(8,128)(2,1)} %param.18) | copy-start | bytes 7864324
  383.1 119.8 %copy-start.6 = (bf16[2,5120]{1,0:T(2,128)(2,1)S(1)}, bf16[2,5120]{1,0:T(2,128)(2,1)}, u32[]{:S(2)}) copy-start(bf16[2,5120]{1,0:T(2,128)(2,1)} %param.24) | copy-start | bytes 61444
where the time goes:
time: 509 us; the launch traced here: 504 us
  waiting for transfers between devices  269 us (53%)
  local copies, waits for them, and re-layouts  62.1 us (12%)
  blocking collectives  58.6 us (12%)
  starting transfers between devices  54 us (11%)
  other arithmetic  41.9 us (8%)
  matrix products  17.5 us (3%)
    all_to_all x3, waiting for transfers between devices, sum_in_two_steps(): lax.all_to_all(nearer, far, split_axis=0, concat_axis=0, tiled=True)  230 us
    all_to_all x2, blocking collectives, sent_to_all(): lax.all_to_all(jnp.broadcast_to(value[None], (length, *value.shape)), axi...  36 us
    all_to_all x2, waiting for transfers between devices, sent_to_all(): lax.all_to_all(jnp.broadcast_to(value[None], (length, *value.shape)), axi...  34.2 us
    all_to_all x3, starting transfers between devices, sum_in_two_steps(): lax.all_to_all(nearer, far, split_axis=0, concat_axis=0, tiled=True)  25 us
    all_to_all x2, blocking collectives, summed_on_arrival(): lax.all_to_all(split_up(value, dim, length), axis, 0, 0, tiled=True)  22.5 us
    all_to_all x2, starting transfers between devices, sent_to_all(): lax.all_to_all(jnp.broadcast_to(value[None], (length, *value.shape)), axi...  22.5 us
    transpose x3, local copies, waits for them, and re-layouts, split_up(): return jnp.moveaxis(blocks, dim, 0)  13.6 us
    reduce_sum x3, other arithmetic, summed_on_arrival(): return jnp.sum(blocks, axis=0)  12.5 us
  transfers between devices with their start and end apart: 6, of which 5 were waited for; matrix products, arithmetic and copies ran while one was open for 13% of the time, Pallas kernels for 0%

commit v1 on v0

v1 whole, which is shorter than its diff:
```python
import functools
import math

import jax
import jax.numpy as jnp
from jax import lax
from jax.experimental import pallas as pl
from jax.experimental.pallas import tpu as pltpu
from jax.sharding import Mesh
from jax.sharding import PartitionSpec as P

HEAD = 128
PIECE = 16
CTX = ("z", "x", "core")
GROUPS_CTX = ("groups", "z", "x", "core")
MESH = pl.DeviceIdType.MESH
MASKED = -1e30
F32 = jnp.float32
BF16 = jnp.bfloat16


def attend_kernel(
    per_step,
    places,
    slot_ref,
    cached_ref,
    act_ref,
    q_ref,
    k_ref,
    v_ref,
    nk_ref,
    nv_ref,
    table_ref,
    num_ref,
    ml_ref,
    gate_ref,
    bias_ref,
    count_ref,
):
    step = pl.program_id(0)
    slots, frames, tokens, _ = k_ref.shape
    sessions, acts = act_ref.shape
    rows = q_ref.shape[0]
    half = rows // 2
    session_rows = rows // sessions
    own = nk_ref.shape[0]
    keys = slots * frames * tokens
    _, nx, nc = places
    factor = math.log2(math.e) / math.sqrt(HEAD)

    @pl.when(step == 0)
    def _():
        pos = (lax.axis_index("z") * nx + lax.axis_index("x")) * nc + lax.axis_index("core")
        key = lax.broadcasted_iota(jnp.int32, (keys, rows), 0)
        row = lax.broadcasted_iota(jnp.int32, (keys, rows), 1)
        live = jnp.zeros((keys, rows), jnp.int32)
        for s in range(sessions):
            count = jnp.clip(cached_ref[s] - pos * frames, 0, frames) * tokens
            base = slot_ref[s] * (frames * tokens)
            here = (row >= s * session_rows) & (row < (s + 1) * session_rows)
            live = jnp.where(here & (key >= base) & (key < base + count), 1, live)
        bias_ref[0:keys, :] = jnp.where(live == 1, 0.0, MASKED)
        key = lax.broadcasted_iota(jnp.int32, (PIECE, rows), 0)
        row = lax.broadcasted_iota(jnp.int32, (PIECE, rows), 1)
        first = pos * own
        session = first // session_rows
        low = session * session_rows
        good = (row >= low) & (row < low + session_rows) & (key < own)
        good = good & (((row - first - key) & 1) == 0)
        bias_ref[keys : keys + PIECE, :] = jnp.where(good, 0.0, MASKED)
        vocab = table_ref.shape[0]
        lane = lax.broadcasted_iota(jnp.int32, (8, vocab), 1)
        sums = jnp.zeros((8, vocab), F32)
        for a in range(acts):
            sums = sums + jnp.where(lane == act_ref[session, a], 1.0, 0.0)
        count_ref[...] = sums

    spot = lax.broadcasted_iota(jnp.int32, (PIECE, HEAD), 0)

    def few(ref, cols):
        values = jnp.zeros((PIECE, HEAD), F32)
        for j in range(own):
            values = jnp.where(spot == j, ref[j : j + 1, cols].astype(F32), values)
        return values.astype(BF16)

    last = (((1,), (1,)), ((), ()))
    first_dims = (((0,), (0,)), ((), ()))
    for i in range(per_step):
        cols = slice(i * HEAD, (i + 1) * HEAD)
        q = q_ref[:, cols]
        k = k_ref[:, :, :, cols].reshape(keys, HEAD)
        v = v_ref[:, :, :, cols].reshape(keys, HEAD)
        s1 = lax.dot_general(k, q, last, preferred_element_type=F32)
        s2 = lax.dot_general(few(nk_ref, cols), q, last, preferred_element_type=F32)
        s1 = s1 * factor + bias_ref[0:keys, :]
        s2 = s2 * factor + bias_ref[keys : keys + PIECE, :]
        top = jnp.maximum(jnp.max(s1, 0, keepdims=True), jnp.max(s2, 0, keepdims=True))
        p1 = jnp.exp2(s1 - top)
        p2 = jnp.exp2(s2 - top)
        total = jnp.sum(p1, 0, keepdims=True) + jnp.sum(p2, 0, keepdims=True)
        numer = lax.dot_general(v, p1.astype(BF16), first_dims, preferred_element_type=F32)
        numer = numer + lax.dot_general(
            few(nv_ref, cols), p2.astype(BF16), first_dims, preferred_element_type=F32
        )
        numer = numer.astype(num_ref.dtype)
        head = step * per_step + i
        for c in range(2):
            part = slice(c * half, (c + 1) * half)
            num_ref[c, cols, :] = numer[:, part]
            ml_ref[c, 0, pl.ds(head, 1), :] = top[:, part]
            ml_ref[c, 1, pl.ds(head, 1), :] = total[:, part]
    sums = jnp.dot(count_ref[...].astype(BF16), table_ref[...], preferred_element_type=F32)
    gate_ref[...] = 1.0 + sums[0:1, :] / acts


def attend(queries, nk, nv, keys, values, slot_of, cached, actions, table, places):
    rows, model_dim = queries.shape
    heads = model_dim // HEAD
    per_step = 4 if heads % 4 == 0 else 1
    width = per_step * HEAD
    slots, frames, tokens, _ = keys.shape
    own = nk.shape[0]
    vocab = table.shape[0]
    flat = lambda n: pl.BlockSpec((n, width), lambda i, *_: (0, i))
    block = pl.BlockSpec((slots, frames, tokens, width), lambda i, *_: (0, 0, 0, i))
    half = rows // 2
    return pl.pallas_call(
        functools.partial(attend_kernel, per_step, places),
        grid_spec=pltpu.PrefetchScalarGridSpec(
            num_scalar_prefetch=3,
            grid=(heads // per_step,),
            in_specs=[flat(rows), block, block, flat(own), flat(own), flat(vocab)],
            out_specs=[
                pl.BlockSpec((2, width, half), lambda i, *_: (0, i, 0)),
                pl.BlockSpec((2, 2, heads, half), lambda i, *_: (0, 0, 0, 0)),
                flat(1),
            ],
            scratch_shapes=[
                pltpu.VMEM((slots * frames * tokens + PIECE, rows), F32),
                pltpu.VMEM((8, vocab), F32),
            ],
        ),
        out_shape=[
            jax.ShapeDtypeStruct((2, model_dim, half), BF16),
            jax.ShapeDtypeStruct((2, 2, heads, half), F32),
            jax.ShapeDtypeStruct((1, model_dim), F32),
        ],
        compiler_params=pltpu.CompilerParams(dimension_semantics=("arbitrary",)),
        name="attend",
    )(slot_of, cached, actions, queries, keys, values, nk, nv, table)


def join_kernel(places, lag, num_ref, ml_ref, w_ref, gate_ref, null_ref, res_ref, out_ref, *rest):
    (
        mlr, scale, joint, ra, d, rel, relout, fin1, fin2, xs, zr, zms, zmr, fz, acc,
        attg, wbuf, pr, prr, fin, finr,
        ml_s, ml_r, a_s, a_r, o_s, o_r, d_s, d_r, r_s, r_r, z_s, z_r, zm_s, zm_r,
        at_s, at_r, w_s, w_r, p_s, p_r, f_s, f_r,
    ) = rest
    nz, nx, nc = places
    near = nx * nc
    z, x, c = (lax.axis_index(name) for name in CTX)
    me = x * nc + c
    heads = ml_ref.shape[2]
    model_dim = num_ref.shape[1]
    wide = model_dim // nz
    blk = wide // nx
    pieces = blk // PIECE
    per_head = HEAD // PIECE
    cols = model_dim // near
    wrows = w_ref.shape[0]

    def near_id(j):
        return {"x": j // nc, "core": lax.rem(j, nc)}

    def send(src, dst, ssem, rsem, where):
        copy = pltpu.make_async_remote_copy(
            src_ref=src, dst_ref=dst, send_sem=ssem, recv_sem=rsem,
            device_id=where, device_id_type=MESH,
        )
        copy.start()

    def got(dst, sem):
        pltpu.make_async_remote_copy(
            src_ref=dst, dst_ref=dst, send_sem=sem, recv_sem=sem,
            device_id={"core": 1 - c}, device_id_type=MESH,
        ).wait_recv()

    def gone(src, sem):
        pltpu.make_async_remote_copy(
            src_ref=src, dst_ref=src, send_sem=sem, recv_sem=sem,
            device_id={"core": 1 - c}, device_id_type=MESH,
        ).wait_send()

    def near_peer(i):
        return lax.rem(me + i, near)

    def far_peer(i):
        return lax.rem(z + i, nz)

    barrier = pltpu.get_barrier_semaphore()

    @pl.loop(1, near)
    def _(i):
        pl.semaphore_signal(barrier, inc=1, device_id=near_id(near_peer(i)), device_id_type=MESH)

    @pl.loop(1, nz)
    def _(i):
        pl.semaphore_signal(barrier, inc=1, device_id={"z": far_peer(i)}, device_id_type=MESH)

    pl.semaphore_wait(barrier, near + nz - 2)

    def turn(k):
        odd = lax.rem(k, 2)
        ahead = nz // 2 + odd * ((k + 1) // 2) - (1 - odd) * (k // 2)
        return lax.rem(z + ahead, nz)

    @pl.loop(1, near)
    def _(i):
        j = near_peer(i)
        send(ml_ref.at[lax.rem(j, nc)], mlr.at[me], ml_s.at[j], ml_r.at[me], near_id(j))

    @pl.loop(0, nz)
    def _(k):
        t = turn(k)
        part = pl.ds(pl.multiple_of(t * wide, PIECE), wide)
        send(num_ref.at[1 - c, part], ra.at[part], a_s.at[t], a_r.at[t], {"core": 1 - c})

    mlr[me] = ml_ref[c]

    @pl.loop(1, near)
    def _(i):
        j = near_peer(i)
        got(mlr.at[j], ml_r.at[j])

    top = mlr[0, 0]
    for j in range(1, near):
        top = jnp.maximum(top, mlr[j, 0])
    total = jnp.zeros_like(top)
    for j in range(near):
        total = total + mlr[j, 1] * jnp.exp2(mlr[j, 0] - top)
    scale[0] = jnp.exp2(ml_ref[c, 0] - top)
    scale[1] = jnp.exp2(mlr[x * nc + 1 - c, 0] - top)
    joint[0] = top
    joint[1] = total

    @pl.loop(0, nz)
    def _(t):
        low = (t * (wide // PIECE) + x * pieces) // per_head
        high = jnp.minimum(low + 1, heads - 1)
        zms[t, 0:1, :] = joint[0, pl.ds(low, 1), :]
        zms[t, 1:2, :] = joint[0, pl.ds(high, 1), :]
        zms[t, 2:3, :] = joint[1, pl.ds(low, 1), :]
        zms[t, 3:4, :] = joint[1, pl.ds(high, 1), :]
        zms[t, 4:8, :] = jnp.zeros((4, zms.shape[2]), F32)

    @pl.loop(1, nz)
    def _(i):
        t = far_peer(i)
        send(zms.at[t], zmr.at[z], zm_s.at[t], zm_r.at[z], {"z": t})

    def ways(t):
        back = lax.rem(t, 2)
        ahead = lax.rem(x + 1 + (nx - 2) * back, nx)
        behind = lax.rem(x + nx - 1 - (nx - 2) * back, nx)
        return ahead, behind

    opposite = lax.rem(x + nx // 2, nx)

    def rows_of(t, xx):
        return pl.ds(pl.multiple_of(t * wide + xx * blk, PIECE), blk)

    def merge(k):
        t = turn(k)
        part = pl.ds(pl.multiple_of(t * wide, PIECE), wide)
        got(ra.at[part], a_r.at[t])
        for i in range(wide // PIECE):
            g = t * (wide // PIECE) + i
            h = g // per_head
            r = pl.ds(pl.multiple_of(g * PIECE, PIECE), PIECE)
            mine = num_ref[c, r, :].astype(F32) * scale[0, pl.ds(h, 1), :]
            other = ra[r, :].astype(F32) * scale[1, pl.ds(h, 1), :]
            d[r, :] = (mine + other).astype(BF16)
        ahead, behind = ways(t)
        send(d.at[rows_of(t, opposite)], rel.at[t], o_s.at[t], o_r.at[t], {"x": ahead})
        send(d.at[rows_of(t, behind)], fin2.at[t], d_s.at[t], d_r.at[t], {"x": behind})

    def relay(k):
        t = turn(k)
        ahead, _ = ways(t)
        got(rel.at[t], o_r.at[t])
        relout[t] = (rel[t].astype(F32) + d[rows_of(t, ahead), :].astype(F32)).astype(BF16)
        send(relout.at[t], fin1.at[t], r_s.at[t], r_r.at[t], {"x": ahead})

    def settle(k):
        t = turn(k)
        got(fin1.at[t], r_r.at[t])
        got(fin2.at[t], d_r.at[t])
        sums = fin1[t].astype(F32) + fin2[t].astype(F32) + d[rows_of(t, x), :].astype(F32)
        xs[t] = sums.astype(BF16)

        @pl.when(k < nz - 1)
        def _():
            send(xs.at[t], zr.at[z], z_s.at[t], z_r.at[z], {"z": t})

    @pl.loop(0, nz + 2 * lag)
    def _(k):
        @pl.when(k < nz)
        def _():
            merge(k)

        @pl.when((k >= lag) & (k < nz + lag))
        def _():
            relay(k - lag)

        @pl.when(k >= 2 * lag)
        def _():
            settle(k - 2 * lag)

    def wpart(j):
        return pl.ds(pl.multiple_of(j * cols, cols), cols)

    @pl.loop(1, near)
    def _(i):
        j = near_peer(i)
        send(w_ref.at[:, wpart(j)], wbuf.at[me], w_s.at[j], w_r.at[me], near_id(j))

    wbuf[me] = w_ref[:, wpart(me)]
    zr[z] = xs[z]
    zmr[z] = zms[z]

    @pl.loop(1, nz)
    def _(i):
        t = far_peer(i)
        got(zmr.at[t], zm_r.at[t])

    top = zmr[0, 0:2, :]
    for t in range(1, nz):
        top = jnp.maximum(top, zmr[t, 0:2, :])
    total = jnp.zeros_like(top)
    for t in range(nz):
        total = total + zmr[t, 2:4, :] * jnp.exp2(zmr[t, 0:2, :] - top)
    for t in range(nz):
        fz[t, 0:2, :] = jnp.exp2(zmr[t, 0:2, :] - top) / total

    first = z * (wide // PIECE) + x * pieces
    low = first // per_head
    acc[...] = jnp.zeros_like(acc)

    @pl.loop(0, nz)
    def _(i):
        t = far_peer(i)

        @pl.when(i > 0)
        def _():
            got(zr.at[t], z_r.at[t])

        for n in range(pieces):
            r = slice(n * PIECE, (n + 1) * PIECE)
            which = (first + n) // per_head - low
            acc[r, :] = acc[r, :] + zr[t, r, :].astype(F32) * fz[t, pl.ds(which, 1), :]

    for n in range(nc):
        attg[me, n] = acc[n * wrows : (n + 1) * wrows, :].astype(BF16)

    @pl.loop(1, near)
    def _(i):
        j = near_peer(i)
        send(attg.at[me], attg.at[me], at_s.at[j], at_r.at[me], near_id(j))

    @pl.loop(1, near)
    def _(i):
        j = near_peer(i)
        got(wbuf.at[j], w_r.at[j])

    @pl.loop(1, near)
    def _(i):
        j = near_peer(i)
        got(attg.at[j], at_r.at[j])

    share = nz // nc
    for cc in range(nc):
        product = None
        for xx in range(nx):
            for n in range(nc):
                term = lax.dot_general(
                    attg[xx * nc + cc, n], wbuf[xx * nc + n], (((0,), (0,)), ((), ())),
                    preferred_element_type=F32,
                )
                product = term if product is None else product + term
        pr[cc * share : (cc + 1) * share] = product.astype(BF16).reshape(share, -1, cols)

    @pl.loop(1, nz)
    def _(i):
        t = far_peer(i)
        send(pr.at[t], prr.at[z], p_s.at[t], p_r.at[z], {"z": t})

    prr[z] = pr[z]

    @pl.loop(1, nz)
    def _(i):
        t = far_peer(i)
        got(prr.at[t], p_r.at[t])

    sums = prr[0].astype(F32)
    for t in range(1, nz):
        sums = sums + prr[t].astype(F32)
    own = res_ref.shape[0]
    for j in range(near):
        fin[j] = sums[j * own : (j + 1) * own, :]

    @pl.loop(1, near)
    def _(i):
        j = near_peer(i)
        send(fin.at[j], finr.at[me], f_s.at[j], f_r.at[me], near_id(j))

    finr[me] = fin[me]

    @pl.loop(1, near)
    def _(i):
        j = near_peer(i)
        got(finr.at[j], f_r.at[j])

    even = (lax.broadcasted_iota(jnp.int32, (own, cols), 0) & 1) == 0
    for j in range(near):
        part = slice(j * cols, (j + 1) * cols)
        gates = jnp.where(even, gate_ref[:, part], 1.0 + null_ref[:, part])
        out_ref[:, part] = (res_ref[:, part].astype(F32) + gates * finr[j]).astype(BF16)

    @pl.loop(1, near)
    def _(i):
        j = near_peer(i)
        gone(ml_ref.at[0], ml_s.at[j])
        gone(wbuf.at[0], w_s.at[j])
        gone(attg.at[0], at_s.at[j])
        gone(fin.at[0], f_s.at[j])

    @pl.loop(0, nz)
    def _(t):
        gone(ra.at[pl.ds(0, wide)], a_s.at[t])
        gone(rel.at[0], o_s.at[t])
        gone(fin2.at[0], d_s.at[t])
        gone(relout.at[0], r_s.at[t])

    @pl.loop(1, nz)
    def _(i):
        t = far_peer(i)
        gone(zms.at[0], zm_s.at[t])
        gone(xs.at[0], z_s.at[t])
        gone(pr.at[0], p_s.at[t])


def join(numer, ml, weight, gate, null_gate, residual, places):
    nz, nx, nc = places
    near = nx * nc
    _, model_dim, half = numer.shape
    heads = ml.shape[2]
    wide = model_dim // nz
    blk = wide // nx
    cols = model_dim // near
    own = residual.shape[0]
    vmem = pl.BlockSpec(memory_space=pltpu.VMEM)
    dma = lambda n: pltpu.SemaphoreType.DMA((n,))
    band = 2 * half // nz
    blocks = pltpu.VMEM((nz, blk, half), BF16)
    scratch = [
        pltpu.VMEM((near, 2, heads, half), F32),
        pltpu.VMEM((2, heads, half), F32),
        pltpu.VMEM((2, heads, half), F32),
        pltpu.VMEM((model_dim, half), BF16),
        pltpu.VMEM((model_dim, half), BF16),
        blocks, blocks, blocks, blocks, blocks, blocks,
        pltpu.VMEM((nz, 8, half), F32),
        pltpu.VMEM((nz, 8, half), F32),
        pltpu.VMEM((nz, 8, half), F32),
        pltpu.VMEM((blk, half), F32),
        pltpu.VMEM((near, nc, weight.shape[0], half), BF16),
        pltpu.VMEM((near, weight.shape[0], cols), BF16),
        pltpu.VMEM((nz, band, cols), BF16),
        pltpu.VMEM((nz, band, cols), BF16),
        pltpu.VMEM((near, own, cols), F32),
        pltpu.VMEM((near, own, cols), F32),
    ]
    for size in (near, nz, nz, nz, nz, nz, nz, near, near, nz, near):
        scratch += [dma(size), dma(size)]
    return pl.pallas_call(
        functools.partial(join_kernel, places, min(4, nz)),
        out_shape=jax.ShapeDtypeStruct(residual.shape, BF16),
        in_specs=[vmem] * 6,
        out_specs=vmem,
        scratch_shapes=scratch,
        compiler_params=pltpu.CompilerParams(
            collective_id=0, has_side_effects=True, vmem_limit_bytes=48 << 20
        ),
        name="join",
    )(numer, ml, weight, gate, null_gate, residual)


def solution(mesh):
    places = (16, 4, 2)
    split = Mesh(mesh.devices.reshape(mesh.shape["groups"], *places), GROUPS_CTX)

    def on_device(
        queries, new_keys, new_values, cache_keys, cache_values, slot_of, cached, actions,
        action_table, null_gate, residual, out_weight,
    ):
        numer, ml, gate = attend(
            queries, new_keys, new_values, cache_keys, cache_values, slot_of, cached, actions,
            action_table, places,
        )
        return join(numer, ml, out_weight, gate, null_gate[None, :], residual, places)

    in_specs = (
        P("groups", None),
        P(GROUPS_CTX, None),
        P(GROUPS_CTX, None),
        P("groups", CTX, None, None),
        P("groups", CTX, None, None),
        P("groups"),
        P("groups"),
        P("groups", None),
        P(),
        P(),
        P(GROUPS_CTX, None),
        P(CTX, None),
    )
    return jax.shard_map(
        on_device, mesh=split, in_specs=in_specs, out_specs=P(GROUPS_CTX, None), check_vma=False
    )
```

time: 509 us -> 108 us (0.21)
  waiting for transfers between devices: 269 us -> 0 us
  Pallas kernels: 0 us -> 103 us
  blocking collectives: 58.6 us -> 0 us
  local copies, waits for them, and re-layouts: 62.1 us -> 3.97 us
  starting transfers between devices: 54 us -> 0 us
  other arithmetic: 41.9 us -> 0 us
  matrix products: 17.5 us -> 0 us
    all_to_all x6 -> x0, waiting for transfers between devices: 269 us -> none  [the longest x3 230 us: sum_in_two_steps(): lax.all_to_all(nearer, far, split_axis=0, concat_axis=0, tiled=True)]
    pallas_call x0 -> x2, Pallas kernels: none -> 103 us  [the longest x1 87.4 us: join(): pl.pallas_call(functools.partial(join_kernel, places, min(4, nz)), out_sh...]
    all_to_all x4 -> x0, blocking collectives: 58.6 us -> none  [the longest x2 36 us: sent_to_all(): lax.all_to_all(jnp.broadcast_to(value[None], (length, *value.shape)), axi...]
    all_to_all x6 -> x0, starting transfers between devices: 54 us -> none  [the longest x3 25 us: sum_in_two_steps(): lax.all_to_all(nearer, far, split_axis=0, concat_axis=0, tiled=True)]
    reduce_sum x9 -> x0, other arithmetic: 21.3 us -> none  [the longest x3 12.5 us: summed_on_arrival(): return jnp.sum(blocks, axis=0)]
    transpose x9 -> x0, local copies, waits for them, and re-layouts: 19.3 us -> none  [the longest x3 13.6 us: split_up(): return jnp.moveaxis(blocks, dim, 0)]
    dot_general x6 -> x0, matrix products: 17.5 us -> none  [the longest x1 4.07 us: on_device(): jnp.einsum('shqk,skhd->sqhd', cache_weights.astype(jnp.bfloat16), slot_va...]
    reshape x5 -> x0, local copies, waits for them, and re-layouts: 17 us -> none  [the longest x1 8.76 us: on_device(): cache_numer = jnp.einsum('shqk,skhd->sqhd', cache_weights.astype(jnp.bflo...]
  transfers between devices with their start and end apart: 6 -> 0, of which waited for: 5 -> 0; matrix products, arithmetic and copies ran while one was open for 13% -> 0% of each run, Pallas kernels for 0% -> 0%
where the time goes in v1:
time: 108 us; the launch traced here: 107 us
  Pallas kernels  103 us (95%)
  local copies, waits for them, and re-layouts  3.97 us (4%)
    pallas_call x1, Pallas kernels, join(): pl.pallas_call(functools.partial(join_kernel, places, min(4, nz)), out_sh...  87.4 us
    pallas_call x1, Pallas kernels, attend(): pl.pallas_call(functools.partial(attend_kernel, per_step, places), grid_s...  15.6 us
    unnamed x13, local copies, waits for them, and re-layouts  3.97 us

profile of v1, /device:TPU:33, one launch (start us, length us, event | category | flops | bytes accessed | tf_op | source)
XLA Modules:
  0.0 107.1 jit_solution(13626806579121445087)
XLA Ops:
  0.0 0.0 copy-start.1
  0.0 0.0 copy-start.3
  0.0 0.0 copy-start.4
  0.0 15.6 %attend.1 = (bf16[2,5120,128]{2,1,0:T(8,128)(2,1)}, f32[2,2,40,128]{3,2,1,0:T(8,128)}, f32[1,5120]{1,0:T(1,128)}) custom-call(s32[4]{0:T(128)} %slot_ref.1, s32[4]{0:T(128)} %cached_ref.1, s32[4,8]{1,0:T(4,128)} %act_ref.1, bf16[256,5120]{1,0:T(8,128)(2,1)} %q_ref.1, bf16[4,2,32,5120]{3,2,1,0:T(8,128)(2,1)} %k_ref.1, bf16[4,2,32,5120]{3,2,1,0:T(8,128)(2,1)} %v_ref.1, ...), custom_call_target="tpu_custom_call" | custom-call | tf_op jit(solution)/shard_map/attend/pallas_call | solution.py:127
  15.7 0.0 copy-done.1
  15.7 0.0 copy-done.3
  15.7 0.0 copy-done.4
  15.7 0.0 copy-start
  15.7 1.7 %copy-done = bf16[2,5120,128]{2,1,0:T(8,128)(2,1)S(1)} copy-done((bf16[2,5120,128]{2,1,0:T(8,128)(2,1)S(1)}, bf16[2,5120,128]{2,1,0:T(8,128)(2,1)}, u32[]{:S(2)}) %copy-start) | copy-done | bytes 2621464
  17.4 0.0 copy-start.2
  17.4 0.9 copy-done.2
  18.3 0.0 copy-start.5
  18.3 0.7 copy-done.5
  19.0 87.4 %join.1 = bf16[2,5120]{1,0:T(2,128)(2,1)S(1)} custom-call(bf16[2,5120,128]{2,1,0:T(8,128)(2,1)S(1)} %copy-done, f32[2,2,40,128]{3,2,1,0:T(8,128)S(1)} %copy-done.2, bf16[40,5120]{1,0:T(8,128)(2,1)S(1)} %copy-done.1, f32[1,5120]{1,0:T(1,128)S(1)} %copy-done.5, f32[1,5120]{1,0:T(1,128)S(1)} %bitcast.1, bf16[2,5120]{1,0:T(2,128)(2,1)S(1)} %copy-done.4), custom_call_target="tpu_custom_call" | custom-call | tf_op jit(solution)/shard_map/join/pallas_call | solution.py:486
  106.5 0.6 copy.14
Async XLA Ops:
  0.0 15.7 %copy-start.1 = (bf16[40,5120]{1,0:T(8,128)(2,1)S(1)}, bf16[40,5120]{1,0:T(8,128)(2,1)}, u32[]{:S(2)}) copy-start(bf16[40,5120]{1,0:T(8,128)(2,1)} %w_ref.1) | copy-start | bytes 1228804
  0.0 15.7 %copy-start.3 = (f32[5120]{0:T(1024)S(1)}, f32[5120]{0:T(1024)}, u32[]{:S(2)}) copy-start(f32[5120]{0:T(1024)} %param.21) | copy-start | bytes 61444
  0.0 15.7 %copy-start.4 = (bf16[2,5120]{1,0:T(2,128)(2,1)S(1)}, bf16[2,5120]{1,0:T(2,128)(2,1)}, u32[]{:S(2)}) copy-start(bf16[2,5120]{1,0:T(2,128)(2,1)} %res_ref.1) | copy-start | bytes 61444
  15.7 1.7 %copy-start = (bf16[2,5120,128]{2,1,0:T(8,128)(2,1)S(1)}, bf16[2,5120,128]{2,1,0:T(8,128)(2,1)}, u32[]{:S(2)}) copy-start(bf16[2,5120,128]{2,1,0:T(8,128)(2,1)} %get-tuple-element.8.num_ref) | copy-start | bytes 7864324
  17.4 0.9 copy-start.2
  18.3 0.7 copy-start.5

commit v2 on v0

v2 whole, which is shorter than its diff:
```python
import functools
import math

import jax
import jax.numpy as jnp
from jax import lax
from jax.experimental import pallas as pl
from jax.experimental.pallas import tpu as pltpu
from jax.sharding import Mesh
from jax.sharding import PartitionSpec as P

HEAD = 128
PIECE = 16
CTX = ("z", "x", "core")
GROUPS_CTX = ("groups", "z", "x", "core")
MESH = pl.DeviceIdType.MESH
MASKED = -1e30
F32 = jnp.float32
BF16 = jnp.bfloat16
LAST = (((1,), (1,)), ((), ()))
FIRST = (((0,), (0,)), ((), ()))


def kernel(places, per_step, lag, *refs):
    (
        slot_ref, cached_ref, act_ref, q_ref, k_ref, v_ref, nk_ref, nv_ref, table_ref,
        w_ref, null_ref, res_ref, out_ref,
        bias, count, gate, away, home, ml, mlp, scale, joint, mlx, ratio,
        ra, d, rel, relout, fin1, fin2, xs, zr, zms, zmr, fz, acc,
        wn, att, attg, wbuf, pr, prr, fin, finr,
        ml_s, ml_r, mx_s, mx_r, a_s, a_r, o_s, o_r, d_s, d_r, r_s, r_r, z_s, z_r, zm_s, zm_r,
        wn_s, wn_r, at_s, at_r, w_s, w_r, p_s, p_r, f_s, f_r,
    ) = refs
    nz, nx, nc = places
    near = nx * nc
    z, x, c = (lax.axis_index(name) for name in CTX)
    me = x * nc + c
    other = 1 - c
    step = pl.program_id(0)
    steps = pl.num_programs(0)
    _, frames, tokens, _ = k_ref.shape
    sessions, acts = act_ref.shape
    rows = q_ref.shape[0]
    half = rows // nc
    session_rows = rows // sessions
    mine = sessions // nc
    slot_keys = frames * tokens
    keys = mine * slot_keys
    own = nk_ref.shape[0]
    model_dim = w_ref.shape[1]
    heads = model_dim // HEAD
    wide = model_dim // nz
    blk = wide // nx
    pieces = blk // PIECE
    per_head = HEAD // PIECE
    cols = model_dim // near
    wrows = w_ref.shape[0]
    pos = (z * nx + x) * nc + c
    parity = lax.rem(z, 2)
    twin = z + 1 - 2 * parity
    share = nz // nc
    barrier = pltpu.get_barrier_semaphore()

    def near_id(j):
        return {"x": j // nc, "core": lax.rem(j, nc)}

    def twin_id(j):
        return {"z": twin, "x": j // nc, "core": lax.rem(j, nc)}

    def near_peer(i):
        return lax.rem(me + i, near)

    def far_peer(i):
        return lax.rem(z + i, nz)

    def send(src, dst, ssem, rsem, where):
        pltpu.make_async_remote_copy(
            src_ref=src, dst_ref=dst, send_sem=ssem, recv_sem=rsem,
            device_id=where, device_id_type=MESH,
        ).start()

    def half_copy(ref, sem):
        return pltpu.make_async_remote_copy(
            src_ref=ref, dst_ref=ref, send_sem=sem, recv_sem=sem,
            device_id={"core": other}, device_id_type=MESH,
        )

    def got(ref, sem):
        half_copy(ref, sem).wait_recv()

    def gone(ref, sem):
        half_copy(ref, sem).wait_send()

    def greet(where):
        pl.semaphore_signal(barrier, inc=1, device_id=where, device_id_type=MESH)

    @pl.when(step == 0)
    def _():
        @pl.loop(1, nz)
        def _(i):
            greet({"z": far_peer(i)})

        @pl.loop(1, near)
        def _(i):
            greet(twin_id(near_peer(i)))
            greet(near_id(near_peer(i)))

        key = lax.broadcasted_iota(jnp.int32, (keys, half), 0)
        row = lax.broadcasted_iota(jnp.int32, (keys, half), 1)
        few_key = lax.broadcasted_iota(jnp.int32, (PIECE, half), 0)
        few_row = lax.broadcasted_iota(jnp.int32, (PIECE, half), 1)
        first = pos * own
        session = first // session_rows
        for part in range(nc):
            live = jnp.zeros((keys, half), jnp.int32)
            for s in range(mine):
                alive = cached_ref[part * mine + s] - pos * frames
                alive = jnp.clip(alive, 0, frames) * tokens
                here = (row >= s * session_rows) & (row < (s + 1) * session_rows)
                here = here & (key >= s * slot_keys) & (key < s * slot_keys + alive)
                live = jnp.where(here, 1, live)
            bias[part, 0:keys, :] = jnp.where(live == 1, 0.0, MASKED)
            low = session * session_rows - part * half
            good = (few_row >= low) & (few_row < low + session_rows) & (few_key < own)
            good = good & (((few_row + part * half - first - few_key) & 1) == 0)
            bias[part, keys : keys + PIECE, :] = jnp.where(good, 0.0, MASKED)
        vocab = table_ref.shape[0]
        lane = lax.broadcasted_iota(jnp.int32, (8, vocab), 1)
        sums = jnp.zeros((8, vocab), F32)
        for a in range(acts):
            sums = sums + jnp.where(lane == act_ref[session, a], 1.0, 0.0)
        count[...] = sums

    spot = lax.broadcasted_iota(jnp.int32, (PIECE, HEAD), 0)
    factor = math.log2(math.e) / math.sqrt(HEAD)

    def few(ref, part):
        values = jnp.zeros((PIECE, HEAD), F32)
        for j in range(own):
            values = jnp.where(spot == j, ref[j : j + 1, part].astype(F32), values)
        return values.astype(BF16)

    def taken(ref, extra, part, which):
        parts = []
        for s in range(mine):
            slot = slot_ref[which * mine + s]
            parts.append(ref[slot, :, :, part].reshape(slot_keys, HEAD))
        return jnp.concatenate(parts + [extra], 0)

    for i in range(per_step):
        part = slice(i * HEAD, (i + 1) * HEAD)
        head = step * per_step + i
        place = pl.ds(pl.multiple_of(head * HEAD, HEAD), HEAD)
        few_keys, few_values = few(nk_ref, part), few(nv_ref, part)
        for turn_of in range(nc):
            which = other if turn_of == 0 else c
            q = q_ref[pl.ds(pl.multiple_of(which * half, half), half), part]
            k = taken(k_ref, few_keys, part, which)
            v = taken(v_ref, few_values, part, which)
            s = lax.dot_general(k, q, LAST, preferred_element_type=F32)
            s = s * factor + bias[which]
            top = jnp.max(s, 0, keepdims=True)
            p = jnp.exp2(s - top)
            total = jnp.sum(p, 0, keepdims=True)
            numer = lax.dot_general(v, p.astype(BF16), FIRST, preferred_element_type=F32)
            if turn_of == 0:
                away[place, :] = numer.astype(BF16)
            else:
                home[place, :] = numer
            ml[turn_of, 0, pl.ds(head, 1), :] = top
            ml[turn_of, 1, pl.ds(head, 1), :] = total
    sums = jnp.dot(count[...].astype(BF16), table_ref[...], preferred_element_type=F32)
    width = per_step * HEAD
    spread = pl.ds(pl.multiple_of(step * width, width), width)
    gate[:, spread] = 1.0 + sums[0:1, :] / acts

    def turn(k):
        odd = lax.rem(k, 2)
        ahead = nz // 2 + odd * ((k + 1) // 2) - (1 - odd) * (k // 2)
        return lax.rem(z + ahead, nz)

    def ways(t):
        back = lax.rem(t, 2)
        ahead = lax.rem(x + 1 + (nx - 2) * back, nx)
        behind = lax.rem(x + nx - 1 - (nx - 2) * back, nx)
        return ahead, behind

    opposite = lax.rem(x + nx // 2, nx)

    def rows_of(t, xx):
        return pl.ds(pl.multiple_of(t * wide + xx * blk, PIECE), blk)

    def merge(k):
        t = turn(k)
        got(ra.at[pl.ds(pl.multiple_of(t * wide, PIECE), wide)], a_r.at[t])
        for i in range(wide // PIECE):
            g = t * (wide // PIECE) + i
            h = g // per_head
            r = pl.ds(pl.multiple_of(g * PIECE, PIECE), PIECE)
            here = home[r, :] * scale[0, pl.ds(h, 1), :]
            there = ra[r, :].astype(F32) * scale[1, pl.ds(h, 1), :]
            d[r, :] = (here + there).astype(BF16)
        ahead, behind = ways(t)
        send(d.at[rows_of(t, opposite)], rel.at[t], o_s.at[t], o_r.at[t], {"x": ahead})
        send(d.at[rows_of(t, behind)], fin2.at[t], d_s.at[t], d_r.at[t], {"x": behind})

    def scaled(t, xx, n):
        g = t * (wide // PIECE) + xx * pieces + n
        h = g // per_head
        r = pl.ds(pl.multiple_of(g * PIECE, PIECE), PIECE)
        return h, d[r, :].astype(F32) * ratio[x, pl.ds(h, 1), :]

    def relay(k):
        t = turn(k)
        ahead, behind = ways(t)
        got(rel.at[t], o_r.at[t])
        for n in range(pieces):
            h, value = scaled(t, ahead, n)
            r = slice(n * PIECE, (n + 1) * PIECE)
            value = value + rel[t, r, :].astype(F32) * ratio[behind, pl.ds(h, 1), :]
            relout[t, r, :] = value.astype(BF16)
        send(relout.at[t], fin1.at[t], r_s.at[t], r_r.at[t], {"x": ahead})

    def settle(k):
        t = turn(k)
        ahead, _ = ways(t)
        got(fin1.at[t], r_r.at[t])
        got(fin2.at[t], d_r.at[t])
        for n in range(pieces):
            h, value = scaled(t, x, n)
            r = slice(n * PIECE, (n + 1) * PIECE)
            value = value + fin2[t, r, :].astype(F32) * ratio[ahead, pl.ds(h, 1), :]
            xs[t, r, :] = (value + fin1[t, r, :].astype(F32)).astype(BF16)

        @pl.when(k < nz - 1)
        def _():
            send(xs.at[t], zr.at[z], z_s.at[t], z_r.at[z], {"z": t})

    def wpart(j):
        return pl.ds(pl.multiple_of(j * cols, cols), cols)

    def wplace(zz, j):
        return zz * near + j

    @pl.when(step == steps - 1)
    def _():
        pl.semaphore_wait(barrier, nz + 2 * near - 3)

        send(ml.at[0], mlp, ml_s, ml_r, {"core": other})

        @pl.loop(0, nz)
        def _(k):
            t = turn(k)
            part = pl.ds(pl.multiple_of(t * wide, PIECE), wide)
            send(away.at[part], ra.at[part], a_s.at[t], a_r.at[t], {"core": other})

        send(w_ref, wn, wn_s, wn_r, {"z": twin})

        got(mlp, ml_r)
        top = jnp.maximum(ml[1, 0], mlp[0])
        here, there = jnp.exp2(ml[1, 0] - top), jnp.exp2(mlp[0] - top)
        scale[0] = here
        scale[1] = there
        joint[0] = top
        joint[1] = ml[1, 1] * here + mlp[1] * there

        @pl.loop(1, nx)
        def _(i):
            xx = lax.rem(x + i, nx)
            send(joint, mlx.at[x], mx_s.at[xx], mx_r.at[x], {"x": xx})

        mlx[x] = joint[...]

        @pl.loop(0, lag)
        def _(k):
            merge(k)

        @pl.loop(1, nx)
        def _(i):
            xx = lax.rem(x + i, nx)
            got(mlx.at[xx], mx_r.at[xx])

        top = mlx[0, 0]
        for xx in range(1, nx):
            top = jnp.maximum(top, mlx[xx, 0])
        total = jnp.zeros_like(top)
        for xx in range(nx):
            part = jnp.exp2(mlx[xx, 0] - top)
            ratio[xx] = part
            total = total + mlx[xx, 1] * part
        scale2 = mlp
        scale2[0] = top
        scale2[1] = total

        @pl.loop(0, nz)
        def _(t):
            low = (t * (wide // PIECE) + x * pieces) // per_head
            high = jnp.minimum(low + 1, heads - 1)
            zms[t, 0:1, :] = scale2[0, pl.ds(low, 1), :]
            zms[t, 1:2, :] = scale2[0, pl.ds(high, 1), :]
            zms[t, 2:3, :] = scale2[1, pl.ds(low, 1), :]
            zms[t, 3:4, :] = scale2[1, pl.ds(high, 1), :]
            zms[t, 4:8, :] = jnp.zeros((4, half), F32)

        @pl.loop(1, nz)
        def _(i):
            t = far_peer(i)
            send(zms.at[t], zmr.at[z], zm_s.at[t], zm_r.at[z], {"z": t})

        @pl.loop(lag, nz + 2 * lag)
        def _(k):
            @pl.when(k < nz)
            def _():
                merge(k)

            @pl.when(k < nz + lag)
            def _():
                relay(k - lag)

            @pl.when(k >= 2 * lag)
            def _():
                settle(k - 2 * lag)

        got(wn, wn_r)

        @pl.loop(1, near)
        def _(i):
            j = near_peer(i)
            send(
                w_ref.at[:, wpart(j)], wbuf.at[wplace(parity, me)],
                w_s.at[0, j], w_r.at[0, me], near_id(j),
            )
            send(
                wn.at[:, wpart(j)], wbuf.at[wplace(1 - parity, me)],
                w_s.at[1, j], w_r.at[1, me], near_id(j),
            )

        wbuf[wplace(parity, me)] = w_ref[:, wpart(me)]
        wbuf[wplace(1 - parity, me)] = wn[:, wpart(me)]
        zr[z] = xs[z]
        zmr[z] = zms[z]

        @pl.loop(1, nz)
        def _(i):
            t = far_peer(i)
            got(zmr.at[t], zm_r.at[t])

        top = zmr[0, 0:2, :]
        for t in range(1, nz):
            top = jnp.maximum(top, zmr[t, 0:2, :])
        total = jnp.zeros_like(top)
        for t in range(nz):
            total = total + zmr[t, 2:4, :] * jnp.exp2(zmr[t, 0:2, :] - top)
        for t in range(nz):
            fz[t, 0:2, :] = jnp.exp2(zmr[t, 0:2, :] - top) / total

        first = z * (wide // PIECE) + x * pieces
        low = first // per_head
        acc[...] = jnp.zeros_like(acc)

        @pl.loop(0, nz)
        def _(i):
            t = far_peer(i)

            @pl.when(i > 0)
            def _():
                got(zr.at[t], z_r.at[t])

            for n in range(pieces):
                r = slice(n * PIECE, (n + 1) * PIECE)
                which = (first + n) // per_head - low
                acc[r, :] = acc[r, :] + zr[t, r, :].astype(F32) * fz[t, pl.ds(which, 1), :]

        for n in range(nc):
            att[n] = acc[n * wrows : (n + 1) * wrows, :].astype(BF16)

        goal = z - parity + c
        spot_of = parity * nx + x

        @pl.loop(0, near)
        def _(i):
            j = near_peer(i)

            @pl.when((goal != z) | (j != me))
            def _():
                send(
                    att, attg.at[spot_of], at_s.at[j], at_r.at[spot_of],
                    {"z": goal, "x": j // nc, "core": lax.rem(j, nc)},
                )

        @pl.when(goal == z)
        def _():
            attg[spot_of] = att[...]

        @pl.loop(1, near)
        def _(i):
            j = near_peer(i)
            got(wbuf.at[wplace(parity, j)], w_r.at[0, j])
            got(wbuf.at[wplace(1 - parity, j)], w_r.at[1, j])

        @pl.loop(0, near)
        def _(i):
            @pl.when((goal != z) | (i != spot_of))
            def _():
                got(attg.at[i], at_r.at[i])

        product = None
        for i in range(near):
            for n in range(nc):
                term = lax.dot_general(
                    attg[i, n], wbuf[i * nc + n], FIRST, preferred_element_type=F32
                )
                product = term if product is None else product + term
        pr[...] = product.astype(BF16).reshape(share, -1, cols)

        def ahead_of(i):
            return lax.rem(z + i, share)

        @pl.loop(0, share)
        def _(i):
            n = ahead_of(i)
            t = parity * share + n

            @pl.when(t != z)
            def _():
                send(pr.at[n], prr.at[z // nc], p_s.at[n], p_r.at[z // nc], {"z": t})

        @pl.when(z // share == parity)
        def _():
            prr[z // nc] = pr[lax.rem(z, share)]

        @pl.loop(0, share)
        def _(i):
            @pl.when(i * nc + z // share != z)
            def _():
                got(prr.at[i], p_r.at[i])

        sums = prr[0].astype(F32)
        for t in range(1, share):
            sums = sums + prr[t].astype(F32)
        for j in range(near):
            fin[j] = sums[j * own : (j + 1) * own, :]

        @pl.loop(1, near)
        def _(i):
            j = near_peer(i)
            send(fin.at[j], finr.at[me], f_s.at[j], f_r.at[me], near_id(j))

        finr[me] = fin[me]

        @pl.loop(1, near)
        def _(i):
            j = near_peer(i)
            got(finr.at[j], f_r.at[j])

        even = (lax.broadcasted_iota(jnp.int32, (own, cols), 0) & 1) == 0
        for j in range(near):
            part = slice(j * cols, (j + 1) * cols)
            gates = jnp.where(even, gate[:, part], 1.0 + null_ref[:, part])
            out_ref[:, part] = (res_ref[:, part].astype(F32) + gates * finr[j]).astype(BF16)

        gone(mlp, ml_s)
        gone(wn, wn_s)

        @pl.loop(1, nx)
        def _(i):
            gone(joint, mx_s.at[lax.rem(x + i, nx)])

        @pl.loop(1, near)
        def _(i):
            j = near_peer(i)
            gone(wbuf.at[0], w_s.at[0, j])
            gone(wbuf.at[0], w_s.at[1, j])
            gone(fin.at[0], f_s.at[j])

        @pl.loop(0, near)
        def _(j):
            @pl.when((goal != z) | (j != me))
            def _():
                gone(att, at_s.at[j])

        @pl.loop(0, share)
        def _(n):
            @pl.when(parity * share + n != z)
            def _():
                gone(pr.at[0], p_s.at[n])

        @pl.loop(0, nz)
        def _(t):
            gone(ra.at[pl.ds(0, wide)], a_s.at[t])
            gone(rel.at[0], o_s.at[t])
            gone(fin2.at[0], d_s.at[t])
            gone(relout.at[0], r_s.at[t])

        @pl.loop(1, nz)
        def _(i):
            t = far_peer(i)
            gone(zms.at[0], zm_s.at[t])
            gone(xs.at[0], z_s.at[t])


def run(places, slot_of, cached, actions, queries, keys, values, nk, nv, table, w, null, res):
    nz, nx, nc = places
    near = nx * nc
    rows, model_dim = queries.shape
    half = rows // nc
    heads = model_dim // HEAD
    per_step = 4 if heads % 4 == 0 else 1
    width = per_step * HEAD
    slots, frames, tokens, _ = keys.shape
    own = nk.shape[0]
    vocab = table.shape[0]
    wide = model_dim // nz
    blk = wide // nx
    cols = model_dim // near
    wrows = w.shape[0]
    share = nz // nc
    picked = slot_of.shape[0] // nc * frames * tokens + PIECE
    flat = lambda n: pl.BlockSpec((n, width), lambda i: (0, i))
    block = pl.BlockSpec((slots, frames, tokens, width), lambda i: (0, 0, 0, i))
    smem = pl.BlockSpec(memory_space=pltpu.SMEM)
    vmem = pl.BlockSpec(memory_space=pltpu.VMEM)
    dma = lambda *n: pltpu.SemaphoreType.DMA(n)
    f32 = lambda *n: pltpu.VMEM(n, F32)
    bf16 = lambda *n: pltpu.VMEM(n, BF16)
    scratch = [
        f32(nc, picked, half), f32(8, vocab), f32(1, model_dim),
        bf16(model_dim, half), f32(model_dim, half), f32(2, 2, heads, half),
        f32(2, heads, half), f32(2, heads, half), f32(2, heads, half),
        f32(nx, 2, heads, half), f32(nx, heads, half),
        bf16(model_dim, half), bf16(model_dim, half),
        *[bf16(nz, blk, half) for _ in range(6)],
        f32(nz, 8, half), f32(nz, 8, half), f32(nz, 8, half), f32(blk, half),
        bf16(wrows, model_dim), bf16(nc, wrows, half), bf16(near, nc, wrows, half),
        bf16(2 * near, wrows, cols),
        bf16(share, half // share, cols), bf16(share, half // share, cols),
        f32(near, own, cols), f32(near, own, cols),
    ]
    scratch += [pltpu.SemaphoreType.DMA, pltpu.SemaphoreType.DMA]
    for size in (nx, nz, nz, nz, nz, nz, nz):
        scratch += [dma(size), dma(size)]
    scratch += [pltpu.SemaphoreType.DMA, pltpu.SemaphoreType.DMA]
    scratch += [dma(near), dma(near), dma(2, near), dma(2, near)]
    scratch += [dma(share), dma(share), dma(near), dma(near)]
    return pl.pallas_call(
        functools.partial(kernel, places, per_step, min(4, nz)),
        grid=(heads // per_step,),
        in_specs=[smem] * 3 + [flat(rows), block, block, flat(own), flat(own), flat(vocab)] + [vmem] * 3,
        out_specs=vmem,
        out_shape=jax.ShapeDtypeStruct(res.shape, BF16),
        scratch_shapes=scratch,
        compiler_params=pltpu.CompilerParams(
            dimension_semantics=("arbitrary",), collective_id=0, has_side_effects=True,
            vmem_limit_bytes=52 << 20,
        ),
        name="rollout",
    )(slot_of, cached, actions, queries, keys, values, nk, nv, table, w, null, res)


def solution(mesh):
    places = (16, 4, 2)
    split = Mesh(mesh.devices.reshape(mesh.shape["groups"], *places), GROUPS_CTX)

    def on_device(
        queries, new_keys, new_values, cache_keys, cache_values, slot_of, cached, actions,
        action_table, null_gate, residual, out_weight,
    ):
        return run(
            places, slot_of, cached, actions, queries, cache_keys, cache_values, new_keys,
            new_values, action_table, out_weight, null_gate[None, :], residual,
        )

    in_specs = (
        P("groups", None),
        P(GROUPS_CTX, None),
        P(GROUPS_CTX, None),
        P("groups", CTX, None, None),
        P("groups", CTX, None, None),
        P("groups"),
        P("groups"),
        P("groups", None),
        P(),
        P(),
        P(GROUPS_CTX, None),
        P(CTX, None),
    )
    return jax.shard_map(
        on_device, mesh=split, in_specs=in_specs, out_specs=P(GROUPS_CTX, None), check_vma=False
    )
```

time: 509 us -> 95.6 us (0.19)
  waiting for transfers between devices: 269 us -> 0 us
  Pallas kernels: 0 us -> 88.6 us
  blocking collectives: 58.6 us -> 0 us
  local copies, waits for them, and re-layouts: 62.1 us -> 6.51 us
  starting transfers between devices: 54 us -> 0 us
  other arithmetic: 41.9 us -> 0 us
  matrix products: 17.5 us -> 0 us
    all_to_all x6 -> x0, waiting for transfers between devices: 269 us -> none  [the longest x3 230 us: sum_in_two_steps(): lax.all_to_all(nearer, far, split_axis=0, concat_axis=0, tiled=True)]
    pallas_call x0 -> x1, Pallas kernels: none -> 88.6 us  [run(): pl.pallas_call(functools.partial(kernel, places, per_step, min(4, nz)), g...]
    all_to_all x4 -> x0, blocking collectives: 58.6 us -> none  [the longest x2 36 us: sent_to_all(): lax.all_to_all(jnp.broadcast_to(value[None], (length, *value.shape)), axi...]
    all_to_all x6 -> x0, starting transfers between devices: 54 us -> none  [the longest x3 25 us: sum_in_two_steps(): lax.all_to_all(nearer, far, split_axis=0, concat_axis=0, tiled=True)]
    reduce_sum x9 -> x0, other arithmetic: 21.3 us -> none  [the longest x3 12.5 us: summed_on_arrival(): return jnp.sum(blocks, axis=0)]
    transpose x9 -> x0, local copies, waits for them, and re-layouts: 19.3 us -> none  [the longest x3 13.6 us: split_up(): return jnp.moveaxis(blocks, dim, 0)]
    dot_general x6 -> x0, matrix products: 17.5 us -> none  [the longest x1 4.07 us: on_device(): jnp.einsum('shqk,skhd->sqhd', cache_weights.astype(jnp.bfloat16), slot_va...]
    reshape x5 -> x0, local copies, waits for them, and re-layouts: 17 us -> none  [the longest x1 8.76 us: on_device(): cache_numer = jnp.einsum('shqk,skhd->sqhd', cache_weights.astype(jnp.bflo...]
  transfers between devices with their start and end apart: 6 -> 0, of which waited for: 5 -> 0; matrix products, arithmetic and copies ran while one was open for 13% -> 0% of each run, Pallas kernels for 0% -> 0%
where the time goes in v2:
time: 95.6 us; the launch traced here: 95.1 us
  Pallas kernels  88.6 us (93%)
  local copies, waits for them, and re-layouts  6.51 us (7%)
    pallas_call x1, Pallas kernels, run(): pl.pallas_call(functools.partial(kernel, places, per_step, min(4, nz)), g...  88.6 us
    unnamed x17, local copies, waits for them, and re-layouts  6.51 us

profile of v2, /device:TPU:33, one launch (start us, length us, event | category | flops | bytes accessed | tf_op | source)
XLA Modules:
  0.0 95.1 jit_solution(8291203578449195947)
XLA Ops:
  0.0 0.0 copy-start
  0.0 1.0 %copy-done = bf16[40,5120]{1,0:T(8,128)(2,1)S(1)} copy-done((bf16[40,5120]{1,0:T(8,128)(2,1)S(1)}, bf16[40,5120]{1,0:T(8,128)(2,1)}, u32[]{:S(2)}) %copy-start) | copy-done | bytes 409624
  1.0 0.0 copy-start.1
  1.0 0.7 copy-done.1
  1.7 0.0 copy-start.2
  1.7 0.7 copy-done.2
  2.5 0.0 copy-start.3
  2.5 0.7 copy-done.3
  3.2 0.0 copy-start.4
  3.2 0.7 copy-done.4
  3.9 0.0 copy-start.5
  3.9 0.7 copy-done.5
  4.6 0.0 copy-start.6
  4.6 0.7 copy-done.6
  5.3 0.0 copy-start.7
  5.3 0.7 copy-done.7
  5.9 88.6 %rollout.1 = bf16[2,5120]{1,0:T(2,128)(2,1)S(1)} custom-call(s32[4]{0:T(128)S(1)} %copy-done.6, s32[4]{0:T(128)S(1)} %copy-done.7, s32[4,8]{1,0:T(4,128)S(1)} %copy-done.5, bf16[256,5120]{1,0:T(8,128)(2,1)} %refs_3_.1, bf16[4,2,32,5120]{3,2,1,0:T(8,128)(2,1)} %refs_4_.1, bf16[4,2,32,5120]{3,2,1,0:T(8,128)(2,1)} %refs_5_.1, bf16[2,5120]{1,0:T(2,128)(2,1)S(1)} %copy-done.1, ...), custom_call_target="tpu_custom_call" | custom-call | tf_op jit(solution)/shard_map/rollout/pallas_call | solution.py:545
  94.5 0.6 copy.14
Async XLA Ops:
  0.0 1.0 %copy-start = (bf16[40,5120]{1,0:T(8,128)(2,1)S(1)}, bf16[40,5120]{1,0:T(8,128)(2,1)}, u32[]{:S(2)}) copy-start(bf16[40,5120]{1,0:T(8,128)(2,1)} %refs_9_.1) | copy-start | bytes 1228804
  1.0 0.7 copy-start.1
  1.7 0.7 copy-start.2
  2.5 0.7 copy-start.3
  3.2 0.7 copy-start.4
  3.9 0.7 copy-start.5
  4.6 0.7 copy-start.6
  5.3 0.7 copy-start.7

commit v3 on v2

v3 whole, which is shorter than its diff:
```python
import functools
import math

import jax
import jax.numpy as jnp
from jax import lax
from jax.experimental import pallas as pl
from jax.experimental.pallas import tpu as pltpu
from jax.sharding import Mesh
from jax.sharding import PartitionSpec as P

HEAD = 128
PIECE = 16
CTX = ("z", "x", "core")
GROUPS_CTX = ("groups", "z", "x", "core")
MESH = pl.DeviceIdType.MESH
MASKED = -1e30
F32 = jnp.float32
BF16 = jnp.bfloat16
LAST = (((1,), (1,)), ((), ()))
FIRST = (((0,), (0,)), ((), ()))


def kernel(places, per_step, lag, *refs):
    (
        slot_ref, cached_ref, act_ref, q_in, k_in, v_in, nk_in, nv_in, table_in,
        w_in, null_in, res_in, out_ref,
        q_ref, nk_ref, nv_ref, table_ref, w_ref, null_ref, res_ref, k_a, v_a, k_b, v_b, in_s, small_s,
        bias, count, gate, away, home, ml, mlp, scale, joint, mlx, ratio,
        ra, d, rel, relout, fin1, fin2, xs, zr, zms, zmr, fz, acc,
        wn, att, attg, wbuf, pr, prr, fin, finr,
        ml_s, ml_r, mx_s, mx_r, a_s, a_r, o_s, o_r, d_s, d_r, r_s, r_r, z_s, z_r, zm_s, zm_r,
        wn_s, wn_r, at_s, at_r, w_s, w_r, p_s, p_r, f_s, f_r,
    ) = refs
    nz, nx, nc = places
    near = nx * nc
    z, x, c = (lax.axis_index(name) for name in CTX)
    me = x * nc + c
    other = 1 - c
    _, frames, tokens, _ = k_in.shape
    sessions, acts = act_ref.shape
    rows = q_ref.shape[0]
    half = rows // nc
    session_rows = rows // sessions
    mine = sessions // nc
    slot_keys = frames * tokens
    keys = mine * slot_keys
    own = nk_ref.shape[0]
    model_dim = w_ref.shape[1]
    heads = model_dim // HEAD
    wide = model_dim // nz
    blk = wide // nx
    pieces = blk // PIECE
    per_head = HEAD // PIECE
    cols = model_dim // near
    wrows = w_ref.shape[0]
    pos = (z * nx + x) * nc + c
    parity = lax.rem(z, 2)
    twin = z + 1 - 2 * parity
    share = nz // nc
    width = per_step * HEAD
    steps = heads // per_step
    early = k_a.shape[3] // width
    spans = ((0, early, k_a, v_a), (early, steps, k_b, v_b))
    barrier = pltpu.get_barrier_semaphore()

    def near_id(j):
        return {"x": j // nc, "core": lax.rem(j, nc)}

    def twin_id(j):
        return {"z": twin, "x": j // nc, "core": lax.rem(j, nc)}

    def near_peer(i):
        return lax.rem(me + i, near)

    def far_peer(i):
        return lax.rem(z + i, nz)

    def send(src, dst, ssem, rsem, where):
        pltpu.make_async_remote_copy(
            src_ref=src, dst_ref=dst, send_sem=ssem, recv_sem=rsem,
            device_id=where, device_id_type=MESH,
        ).start()

    def half_copy(ref, sem):
        return pltpu.make_async_remote_copy(
            src_ref=ref, dst_ref=ref, send_sem=sem, recv_sem=sem,
            device_id={"core": other}, device_id_type=MESH,
        )

    def got(ref, sem):
        half_copy(ref, sem).wait_recv()

    def gone(ref, sem):
        half_copy(ref, sem).wait_send()

    def greet(where):
        pl.semaphore_signal(barrier, inc=1, device_id=where, device_id_type=MESH)

    @pl.loop(1, nz)
    def _(i):
        greet({"z": far_peer(i)})

    @pl.loop(1, near)
    def _(i):
        greet(twin_id(near_peer(i)))
        greet(near_id(near_peer(i)))

    smalls = (
        (nk_in, nk_ref), (nv_in, nv_ref), (w_in, w_ref), (table_in, table_ref),
        (null_in, null_ref), (res_in, res_ref),
    )

    def small(n):
        return pltpu.make_async_copy(*smalls[n], small_s.at[n])

    def chunk(step, begin, k_to, v_to):
        part = pl.ds(pl.multiple_of(step * width, width), width)
        into = pl.ds(pl.multiple_of((step - begin) * width, width), width)
        return (
            pltpu.make_async_copy(q_in.at[:, part], q_ref.at[:, part], in_s.at[0, step]),
            pltpu.make_async_copy(
                k_in.at[:, :, :, part], k_to.at[:, :, :, into], in_s.at[1, step]
            ),
            pltpu.make_async_copy(
                v_in.at[:, :, :, part], v_to.at[:, :, :, into], in_s.at[2, step]
            ),
        )

    small(0).start()
    small(1).start()

    for begin, end, k_to, v_to in spans:
        @pl.loop(begin, end)
        def _(step):
            for copy in chunk(step, begin, k_to, v_to):
                copy.start()

    for n in range(2, len(smalls)):
        small(n).start()

    key = lax.broadcasted_iota(jnp.int32, (keys, half), 0)
    row = lax.broadcasted_iota(jnp.int32, (keys, half), 1)
    few_key = lax.broadcasted_iota(jnp.int32, (PIECE, half), 0)
    few_row = lax.broadcasted_iota(jnp.int32, (PIECE, half), 1)
    first = pos * own
    session = first // session_rows
    for part in range(nc):
        live = jnp.zeros((keys, half), jnp.int32)
        for s in range(mine):
            alive = cached_ref[part * mine + s] - pos * frames
            alive = jnp.clip(alive, 0, frames) * tokens
            here = (row >= s * session_rows) & (row < (s + 1) * session_rows)
            here = here & (key >= s * slot_keys) & (key < s * slot_keys + alive)
            live = jnp.where(here, 1, live)
        bias[part, 0:keys, :] = jnp.where(live == 1, 0.0, MASKED)
        low = session * session_rows - part * half
        good = (few_row >= low) & (few_row < low + session_rows) & (few_key < own)
        good = good & (((few_row + part * half - first - few_key) & 1) == 0)
        bias[part, keys : keys + PIECE, :] = jnp.where(good, 0.0, MASKED)
    vocab = table_ref.shape[0]
    lane = lax.broadcasted_iota(jnp.int32, (8, vocab), 1)
    sums = jnp.zeros((8, vocab), F32)
    for a in range(acts):
        sums = sums + jnp.where(lane == act_ref[session, a], 1.0, 0.0)
    count[...] = sums

    spot = lax.broadcasted_iota(jnp.int32, (PIECE, HEAD), 0)
    factor = math.log2(math.e) / math.sqrt(HEAD)

    def few(ref, part):
        values = jnp.zeros((PIECE, HEAD), F32)
        for j in range(own):
            values = jnp.where(spot == j, ref[j : j + 1, part].astype(F32), values)
        return values.astype(BF16)

    def taken(ref, extra, part, which):
        parts = []
        for s in range(mine):
            slot = slot_ref[which * mine + s]
            parts.append(ref[slot, :, :, part].reshape(slot_keys, HEAD))
        return jnp.concatenate(parts + [extra], 0)

    small(0).wait()
    small(1).wait()

    def attend(step, i, begin, k_ref, v_ref):
        head = step * per_step + i
        place = pl.ds(pl.multiple_of(head * HEAD, HEAD), HEAD)
        part = place
        into = pl.ds(pl.multiple_of((head - begin * per_step) * HEAD, HEAD), HEAD)
        few_keys, few_values = few(nk_ref, part), few(nv_ref, part)
        for turn_of in range(nc):
            which = other if turn_of == 0 else c
            q = q_ref[pl.ds(pl.multiple_of(which * half, half), half), part]
            k = taken(k_ref, few_keys, into, which)
            v = taken(v_ref, few_values, into, which)
            s = lax.dot_general(k, q, LAST, preferred_element_type=F32)
            s = s * factor + bias[which]
            top = jnp.max(s, 0, keepdims=True)
            p = jnp.exp2(s - top)
            total = jnp.sum(p, 0, keepdims=True)
            numer = lax.dot_general(v, p.astype(BF16), FIRST, preferred_element_type=F32)
            if turn_of == 0:
                away[place, :] = numer.astype(BF16)
            else:
                home[place, :] = numer
            ml[turn_of, 0, pl.ds(head, 1), :] = top
            ml[turn_of, 1, pl.ds(head, 1), :] = total
    for begin, end, k_to, v_to in spans:
        @pl.loop(begin, end)
        def _(step):
            for copy in chunk(step, begin, k_to, v_to):
                copy.wait()

        @pl.loop(begin, end)
        def _(step):
            for i in range(per_step):
                attend(step, i, begin, k_to, v_to)

    small(2).wait()

    def turn(k):
        odd = lax.rem(k, 2)
        ahead = nz // 2 + odd * ((k + 1) // 2) - (1 - odd) * (k // 2)
        return lax.rem(z + ahead, nz)

    def ways(t):
        back = lax.rem(t, 2)
        ahead = lax.rem(x + 1 + (nx - 2) * back, nx)
        behind = lax.rem(x + nx - 1 - (nx - 2) * back, nx)
        return ahead, behind

    opposite = lax.rem(x + nx // 2, nx)

    def rows_of(t, xx):
        return pl.ds(pl.multiple_of(t * wide + xx * blk, PIECE), blk)

    def merge(k):
        t = turn(k)
        got(ra.at[pl.ds(pl.multiple_of(t * wide, PIECE), wide)], a_r.at[t])
        for i in range(wide // PIECE):
            g = t * (wide // PIECE) + i
            h = g // per_head
            r = pl.ds(pl.multiple_of(g * PIECE, PIECE), PIECE)
            here = home[r, :] * scale[0, pl.ds(h, 1), :]
            there = ra[r, :].astype(F32) * scale[1, pl.ds(h, 1), :]
            d[r, :] = (here + there).astype(BF16)
        ahead, behind = ways(t)
        send(d.at[rows_of(t, opposite)], rel.at[t], o_s.at[t], o_r.at[t], {"x": ahead})
        send(d.at[rows_of(t, behind)], fin2.at[t], d_s.at[t], d_r.at[t], {"x": behind})

    def scaled(t, xx, n):
        g = t * (wide // PIECE) + xx * pieces + n
        h = g // per_head
        r = pl.ds(pl.multiple_of(g * PIECE, PIECE), PIECE)
        return h, d[r, :].astype(F32) * ratio[x, pl.ds(h, 1), :]

    def relay(k):
        t = turn(k)
        ahead, behind = ways(t)
        got(rel.at[t], o_r.at[t])
        for n in range(pieces):
            h, value = scaled(t, ahead, n)
            r = slice(n * PIECE, (n + 1) * PIECE)
            value = value + rel[t, r, :].astype(F32) * ratio[behind, pl.ds(h, 1), :]
            relout[t, r, :] = value.astype(BF16)
        send(relout.at[t], fin1.at[t], r_s.at[t], r_r.at[t], {"x": ahead})

    def settle(k):
        t = turn(k)
        ahead, _ = ways(t)
        got(fin1.at[t], r_r.at[t])
        got(fin2.at[t], d_r.at[t])
        for n in range(pieces):
            h, value = scaled(t, x, n)
            r = slice(n * PIECE, (n + 1) * PIECE)
            value = value + fin2[t, r, :].astype(F32) * ratio[ahead, pl.ds(h, 1), :]
            xs[t, r, :] = (value + fin1[t, r, :].astype(F32)).astype(BF16)

        @pl.when(k < nz - 1)
        def _():
            send(xs.at[t], zr.at[z], z_s.at[t], z_r.at[z], {"z": t})

    def wpart(j):
        return pl.ds(pl.multiple_of(j * cols, cols), cols)

    def wplace(zz, j):
        return zz * near + j

    pl.semaphore_wait(barrier, nz + 2 * near - 3)

    send(ml.at[0], mlp, ml_s, ml_r, {"core": other})

    @pl.loop(0, nz)
    def _(k):
        t = turn(k)
        part = pl.ds(pl.multiple_of(t * wide, PIECE), wide)
        send(away.at[part], ra.at[part], a_s.at[t], a_r.at[t], {"core": other})

    send(w_ref, wn, wn_s, wn_r, {"z": twin})

    got(mlp, ml_r)
    top = jnp.maximum(ml[1, 0], mlp[0])
    here, there = jnp.exp2(ml[1, 0] - top), jnp.exp2(mlp[0] - top)
    scale[0] = here
    scale[1] = there
    joint[0] = top
    joint[1] = ml[1, 1] * here + mlp[1] * there

    @pl.loop(1, nx)
    def _(i):
        xx = lax.rem(x + i, nx)
        send(joint, mlx.at[x], mx_s.at[xx], mx_r.at[x], {"x": xx})

    mlx[x] = joint[...]

    @pl.loop(0, lag)
    def _(k):
        merge(k)

    @pl.loop(1, nx)
    def _(i):
        xx = lax.rem(x + i, nx)
        got(mlx.at[xx], mx_r.at[xx])

    top = mlx[0, 0]
    for xx in range(1, nx):
        top = jnp.maximum(top, mlx[xx, 0])
    total = jnp.zeros_like(top)
    for xx in range(nx):
        part = jnp.exp2(mlx[xx, 0] - top)
        ratio[xx] = part
        total = total + mlx[xx, 1] * part
    scale2 = mlp
    scale2[0] = top
    scale2[1] = total

    @pl.loop(0, nz)
    def _(t):
        low = (t * (wide // PIECE) + x * pieces) // per_head
        high = jnp.minimum(low + 1, heads - 1)
        zms[t, 0:1, :] = scale2[0, pl.ds(low, 1), :]
        zms[t, 1:2, :] = scale2[0, pl.ds(high, 1), :]
        zms[t, 2:3, :] = scale2[1, pl.ds(low, 1), :]
        zms[t, 3:4, :] = scale2[1, pl.ds(high, 1), :]
        zms[t, 4:8, :] = jnp.zeros((4, half), F32)

    @pl.loop(1, nz)
    def _(i):
        t = far_peer(i)
        send(zms.at[t], zmr.at[z], zm_s.at[t], zm_r.at[z], {"z": t})

    @pl.loop(lag, nz + 2 * lag)
    def _(k):
        @pl.when(k < nz)
        def _():
            merge(k)

        @pl.when(k < nz + lag)
        def _():
            relay(k - lag)

        @pl.when(k >= 2 * lag)
        def _():
            settle(k - 2 * lag)

    got(wn, wn_r)

    @pl.loop(1, near)
    def _(i):
        j = near_peer(i)
        send(
            w_ref.at[:, wpart(j)], wbuf.at[wplace(parity, me)],
            w_s.at[0, j], w_r.at[0, me], near_id(j),
        )
        send(
            wn.at[:, wpart(j)], wbuf.at[wplace(1 - parity, me)],
            w_s.at[1, j], w_r.at[1, me], near_id(j),
        )

    wbuf[wplace(parity, me)] = w_ref[:, wpart(me)]
    wbuf[wplace(1 - parity, me)] = wn[:, wpart(me)]
    zr[z] = xs[z]
    zmr[z] = zms[z]

    @pl.loop(1, nz)
    def _(i):
        t = far_peer(i)
        got(zmr.at[t], zm_r.at[t])

    top = zmr[0, 0:2, :]
    for t in range(1, nz):
        top = jnp.maximum(top, zmr[t, 0:2, :])
    total = jnp.zeros_like(top)
    for t in range(nz):
        total = total + zmr[t, 2:4, :] * jnp.exp2(zmr[t, 0:2, :] - top)
    for t in range(nz):
        fz[t, 0:2, :] = jnp.exp2(zmr[t, 0:2, :] - top) / total

    first = z * (wide // PIECE) + x * pieces
    low = first // per_head
    acc[...] = jnp.zeros_like(acc)

    @pl.loop(0, nz)
    def _(i):
        t = far_peer(i)

        @pl.when(i > 0)
        def _():
            got(zr.at[t], z_r.at[t])

        for n in range(pieces):
            r = slice(n * PIECE, (n + 1) * PIECE)
            which = (first + n) // per_head - low
            acc[r, :] = acc[r, :] + zr[t, r, :].astype(F32) * fz[t, pl.ds(which, 1), :]

    for n in range(nc):
        att[n] = acc[n * wrows : (n + 1) * wrows, :].astype(BF16)

    goal = z - parity + c
    spot_of = parity * nx + x

    @pl.loop(0, near)
    def _(i):
        j = near_peer(i)

        @pl.when((goal != z) | (j != me))
        def _():
            send(
                att, attg.at[spot_of], at_s.at[j], at_r.at[spot_of],
                {"z": goal, "x": j // nc, "core": lax.rem(j, nc)},
            )

    @pl.when(goal == z)
    def _():
        attg[spot_of] = att[...]

    @pl.loop(1, near)
    def _(i):
        j = near_peer(i)
        got(wbuf.at[wplace(parity, j)], w_r.at[0, j])
        got(wbuf.at[wplace(1 - parity, j)], w_r.at[1, j])

    @pl.loop(0, near)
    def _(i):
        @pl.when((goal != z) | (i != spot_of))
        def _():
            got(attg.at[i], at_r.at[i])

    product = None
    for i in range(near):
        for n in range(nc):
            term = lax.dot_general(
                attg[i, n], wbuf[i * nc + n], FIRST, preferred_element_type=F32
            )
            product = term if product is None else product + term
    pr[...] = product.astype(BF16).reshape(share, -1, cols)

    def ahead_of(i):
        odd = lax.rem(i, 2)
        skew = odd * ((i + 1) // 2) + (1 - odd) * (share - i // 2)
        near_half = jnp.where(z // share == parity, share // 2, 0)
        return lax.rem(z + near_half + skew, share)

    @pl.loop(0, share)
    def _(i):
        n = ahead_of(i)
        t = parity * share + n

        @pl.when(t != z)
        def _():
            send(pr.at[n], prr.at[z // nc], p_s.at[n], p_r.at[z // nc], {"z": t})

    @pl.when(z // share == parity)
    def _():
        prr[z // nc] = pr[lax.rem(z, share)]

    small(3).wait()
    small(4).wait()
    small(5).wait()

    @pl.loop(0, steps)
    def _(step):
        spread = pl.ds(pl.multiple_of(step * width, width), width)
        sums = jnp.dot(count[...].astype(BF16), table_ref[:, spread], preferred_element_type=F32)
        gate[:, spread] = 1.0 + sums[0:1, :] / acts

    @pl.loop(0, share)
    def _(i):
        @pl.when(i * nc + z // share != z)
        def _():
            got(prr.at[i], p_r.at[i])

    sums = prr[0].astype(F32)
    for t in range(1, share):
        sums = sums + prr[t].astype(F32)
    for j in range(near):
        fin[j] = sums[j * own : (j + 1) * own, :]

    @pl.loop(1, near)
    def _(i):
        j = near_peer(i)
        send(fin.at[j], finr.at[me], f_s.at[j], f_r.at[me], near_id(j))

    finr[me] = fin[me]

    @pl.loop(1, near)
    def _(i):
        j = near_peer(i)
        got(finr.at[j], f_r.at[j])

    even = (lax.broadcasted_iota(jnp.int32, (own, cols), 0) & 1) == 0
    for j in range(near):
        part = slice(j * cols, (j + 1) * cols)
        gates = jnp.where(even, gate[:, part], 1.0 + null_ref[:, part])
        out_ref[:, part] = (res_ref[:, part].astype(F32) + gates * finr[j]).astype(BF16)

    gone(mlp, ml_s)
    gone(wn, wn_s)

    @pl.loop(1, nx)
    def _(i):
        gone(joint, mx_s.at[lax.rem(x + i, nx)])

    @pl.loop(1, near)
    def _(i):
        j = near_peer(i)
        gone(wbuf.at[0], w_s.at[0, j])
        gone(wbuf.at[0], w_s.at[1, j])
        gone(fin.at[0], f_s.at[j])

    @pl.loop(0, near)
    def _(j):
        @pl.when((goal != z) | (j != me))
        def _():
            gone(att, at_s.at[j])

    @pl.loop(0, share)
    def _(n):
        @pl.when(parity * share + n != z)
        def _():
            gone(pr.at[0], p_s.at[n])

    @pl.loop(0, nz)
    def _(t):
        gone(ra.at[pl.ds(0, wide)], a_s.at[t])
        gone(rel.at[0], o_s.at[t])
        gone(fin2.at[0], d_s.at[t])
        gone(relout.at[0], r_s.at[t])

    @pl.loop(1, nz)
    def _(i):
        t = far_peer(i)
        gone(zms.at[0], zm_s.at[t])
        gone(xs.at[0], z_s.at[t])


def run(places, slot_of, cached, actions, queries, keys, values, nk, nv, table, w, null, res):
    nz, nx, nc = places
    near = nx * nc
    rows, model_dim = queries.shape
    half = rows // nc
    heads = model_dim // HEAD
    per_step = 4 if heads % 4 == 0 else 1
    _, frames, tokens, _ = keys.shape
    own = nk.shape[0]
    vocab = table.shape[0]
    wide = model_dim // nz
    blk = wide // nx
    cols = model_dim // near
    wrows = w.shape[0]
    share = nz // nc
    picked = slot_of.shape[0] // nc * frames * tokens + PIECE
    smem = pl.BlockSpec(memory_space=pltpu.SMEM)
    vmem = pl.BlockSpec(memory_space=pltpu.VMEM)
    away = pl.BlockSpec(memory_space=pl.ANY)
    dma = lambda *n: pltpu.SemaphoreType.DMA(n)
    f32 = lambda *n: pltpu.VMEM(n, F32)
    bf16 = lambda *n: pltpu.VMEM(n, BF16)
    large = (queries, nk, nv, table, w, null, res)
    scratch = [pltpu.VMEM(value.shape, value.dtype) for value in large]
    steps = heads // per_step
    early = max(1, steps // 5)
    for size in (early, early, steps - early, steps - early):
        scratch.append(bf16(*keys.shape[:3], size * per_step * HEAD))
    scratch += [dma(3, heads // per_step), dma(6)]
    scratch += [
        f32(nc, picked, half), f32(8, vocab), f32(1, model_dim),
        bf16(model_dim, half), f32(model_dim, half), f32(2, 2, heads, half),
        f32(2, heads, half), f32(2, heads, half), f32(2, heads, half),
        f32(nx, 2, heads, half), f32(nx, heads, half),
        bf16(model_dim, half), bf16(model_dim, half),
        *[bf16(nz, blk, half) for _ in range(6)],
        f32(nz, 8, half), f32(nz, 8, half), f32(nz, 8, half), f32(blk, half),
        bf16(wrows, model_dim), bf16(nc, wrows, half), bf16(near, nc, wrows, half),
        bf16(2 * near, wrows, cols),
        bf16(share, half // share, cols), bf16(share, half // share, cols),
        f32(near, own, cols), f32(near, own, cols),
    ]
    scratch += [pltpu.SemaphoreType.DMA, pltpu.SemaphoreType.DMA]
    for size in (nx, nz, nz, nz, nz, nz, nz):
        scratch += [dma(size), dma(size)]
    scratch += [pltpu.SemaphoreType.DMA, pltpu.SemaphoreType.DMA]
    scratch += [dma(near), dma(near), dma(2, near), dma(2, near)]
    scratch += [dma(share), dma(share), dma(near), dma(near)]
    return pl.pallas_call(
        functools.partial(kernel, places, per_step, min(4, nz)),
        in_specs=[smem] * 3 + [away] * 9,
        out_specs=vmem,
        out_shape=jax.ShapeDtypeStruct(res.shape, BF16),
        scratch_shapes=scratch,
        compiler_params=pltpu.CompilerParams(
            collective_id=0, has_side_effects=True, vmem_limit_bytes=67_043_328
        ),
        name="rollout",
    )(slot_of, cached, actions, queries, keys, values, nk, nv, table, w, null, res)


def solution(mesh):
    places = (16, 4, 2)
    split = Mesh(mesh.devices.reshape(mesh.shape["groups"], *places), GROUPS_CTX)

    def on_device(
        queries, new_keys, new_values, cache_keys, cache_values, slot_of, cached, actions,
        action_table, null_gate, residual, out_weight,
    ):
        return run(
            places, slot_of, cached, actions, queries, cache_keys, cache_values, new_keys,
            new_values, action_table, out_weight, null_gate[None, :], residual,
        )

    in_specs = (
        P("groups", None),
        P(GROUPS_CTX, None),
        P(GROUPS_CTX, None),
        P("groups", CTX, None, None),
        P("groups", CTX, None, None),
        P("groups"),
        P("groups"),
        P("groups", None),
        P(),
        P(),
        P(GROUPS_CTX, None),
        P(CTX, None),
    )
    return jax.shard_map(
        on_device, mesh=split, in_specs=in_specs, out_specs=P(GROUPS_CTX, None), check_vma=False
    )
```

time: 95.6 us -> 91.6 us (0.958)
  local copies, waits for them, and re-layouts: 6.51 us -> 1.35 us
  Pallas kernels: 88.6 us -> 90.1 us
    unnamed x17 -> x1, local copies, waits for them, and re-layouts: 6.51 us -> 1.35 us
    pallas_call x1, Pallas kernels: 88.6 us -> 90.1 us  [run(): pl.pallas_call(functools.partial(kernel, places, per_step, min(4, nz)), i...]
where the time goes in v3:
time: 91.6 us; the launch traced here: 91.4 us
  Pallas kernels  90.1 us (98%)
  local copies, waits for them, and re-layouts  1.35 us (1%)
    pallas_call x1, Pallas kernels, run(): pl.pallas_call(functools.partial(kernel, places, per_step, min(4, nz)), i...  90.1 us

profile of v3, /device:TPU:33, one launch (start us, length us, event | category | flops | bytes accessed | tf_op | source)
XLA Modules:
  0.0 91.4 jit_solution(8656674618046446434)
XLA Ops:
  0.0 90.1 %rollout.1 = bf16[2,5120]{1,0:T(2,128)(2,1)} custom-call(s32[4]{0:T(128)} %refs_0_.1, s32[4]{0:T(128)} %refs_1_.1, s32[4,8]{1,0:T(4,128)} %refs_2_.1, bf16[256,5120]{1,0:T(8,128)(2,1)} %refs_3_.1, bf16[4,2,32,5120]{3,2,1,0:T(8,128)(2,1)} %refs_4_.1, bf16[4,2,32,5120]{3,2,1,0:T(8,128)(2,1)} %refs_5_.1, bf16[2,5120]{1,0:T(2,128)(2,1)} %refs_6_.1, ...), custom_call_target="tpu_custom_call" | custom-call | tf_op jit(solution)/shard_map/rollout/pallas_call | solution.py:607
  90.1 1.3 %copy.14 = bf16[2,5120]{1,0:T(2,128)(2,1)} copy(bf16[2,5120]{1,0:T(2,128)(2,1)} %rollout.1) | data formatting | bytes 40960

commit v4 on v3

--- a/solution.py
+++ b/solution.py
@@ -25,7 +25,7 @@
     (
         slot_ref, cached_ref, act_ref, q_in, k_in, v_in, nk_in, nv_in, table_in,
         w_in, null_in, res_in, out_ref,
-        q_ref, nk_ref, nv_ref, table_ref, w_ref, null_ref, res_ref, k_a, v_a, k_b, v_b, in_s, small_s,
+        q_ref, nk_ref, nv_ref, table_ref, w_ref, null_ref, res_ref, k_ref, v_ref, in_s, small_s,
         bias, count, gate, away, home, ml, mlp, scale, joint, mlx, ratio,
         ra, d, rel, relout, fin1, fin2, xs, zr, zms, zmr, fz, acc,
         wn, att, attg, wbuf, pr, prr, fin, finr,
@@ -60,8 +60,6 @@
     share = nz // nc
     width = per_step * HEAD
     steps = heads // per_step
-    early = k_a.shape[3] // width
-    spans = ((0, early, k_a, v_a), (early, steps, k_b, v_b))
     barrier = pltpu.get_barrier_semaphore()
 
     def near_id(j):
@@ -114,30 +112,22 @@
     def small(n):
         return pltpu.make_async_copy(*smalls[n], small_s.at[n])
 
-    def chunk(step, begin, k_to, v_to):
-        part = pl.ds(pl.multiple_of(step * width, width), width)
-        into = pl.ds(pl.multiple_of((step - begin) * width, width), width)
+    def load(n):
+        band = rows // k_in.shape[0]
+        part = pl.ds(pl.multiple_of(n * band, band), band)
         return (
-            pltpu.make_async_copy(q_in.at[:, part], q_ref.at[:, part], in_s.at[0, step]),
-            pltpu.make_async_copy(
-                k_in.at[:, :, :, part], k_to.at[:, :, :, into], in_s.at[1, step]
-            ),
-            pltpu.make_async_copy(
-                v_in.at[:, :, :, part], v_to.at[:, :, :, into], in_s.at[2, step]
-            ),
+            pltpu.make_async_copy(k_in.at[n], k_ref.at[n], in_s.at[0, n]),
+            pltpu.make_async_copy(q_in.at[part], q_ref.at[part], in_s.at[1, n]),
+            pltpu.make_async_copy(v_in.at[n], v_ref.at[n], in_s.at[2, n]),
         )
 
     small(0).start()
     small(1).start()
 
-    for begin, end, k_to, v_to in spans:
-        @pl.loop(begin, end)
-        def _(step):
-            for copy in chunk(step, begin, k_to, v_to):
-                copy.start()
-
-    for n in range(2, len(smalls)):
-        small(n).start()
+    @pl.loop(0, k_in.shape[0])
+    def _(n):
+        for copy in load(n):
+            copy.start()
 
     key = lax.broadcasted_iota(jnp.int32, (keys, half), 0)
     row = lax.broadcasted_iota(jnp.int32, (keys, half), 1)
@@ -184,39 +174,44 @@
     small(0).wait()
     small(1).wait()
 
-    def attend(step, i, begin, k_ref, v_ref):
-        head = step * per_step + i
-        place = pl.ds(pl.multiple_of(head * HEAD, HEAD), HEAD)
-        part = place
-        into = pl.ds(pl.multiple_of((head - begin * per_step) * HEAD, HEAD), HEAD)
-        few_keys, few_values = few(nk_ref, part), few(nv_ref, part)
-        for turn_of in range(nc):
-            which = other if turn_of == 0 else c
-            q = q_ref[pl.ds(pl.multiple_of(which * half, half), half), part]
-            k = taken(k_ref, few_keys, into, which)
-            v = taken(v_ref, few_values, into, which)
-            s = lax.dot_general(k, q, LAST, preferred_element_type=F32)
+    def attend(step):
+        work = []
+        for i in range(per_step):
+            head = step * per_step + i
+            part = pl.ds(pl.multiple_of(head * HEAD, HEAD), HEAD)
+            few_keys = few(nk_ref, part)
+            for which in (other, c):
+                q = q_ref[pl.ds(pl.multiple_of(which * half, half), half), part]
+                k = taken(k_ref, few_keys, part, which)
+                s = lax.dot_general(k, q, LAST, preferred_element_type=F32)
+                work.append((head, part, which, s))
+        ready = []
+        for head, part, which, s in work:
             s = s * factor + bias[which]
             top = jnp.max(s, 0, keepdims=True)
             p = jnp.exp2(s - top)
             total = jnp.sum(p, 0, keepdims=True)
-            numer = lax.dot_general(v, p.astype(BF16), FIRST, preferred_element_type=F32)
-            if turn_of == 0:
-                away[place, :] = numer.astype(BF16)
+            first = 0 if which is other else 1
+            ml[first, 0, pl.ds(head, 1), :] = top
+            ml[first, 1, pl.ds(head, 1), :] = total
+            ready.append((part, which, p.astype(BF16)))
+        for part, which, p in ready:
+            v = taken(v_ref, few(nv_ref, part), part, which)
+            numer = lax.dot_general(v, p, FIRST, preferred_element_type=F32)
+            if which is other:
+                away[part, :] = numer.astype(BF16)
             else:
-                home[place, :] = numer
-            ml[turn_of, 0, pl.ds(head, 1), :] = top
-            ml[turn_of, 1, pl.ds(head, 1), :] = total
-    for begin, end, k_to, v_to in spans:
-        @pl.loop(begin, end)
-        def _(step):
-            for copy in chunk(step, begin, k_to, v_to):
-                copy.wait()
-
-        @pl.loop(begin, end)
-        def _(step):
-            for i in range(per_step):
-                attend(step, i, begin, k_to, v_to)
+                home[part, :] = numer
+
+    for copy in [copy for n in range(k_in.shape[0]) for copy in load(n)]:
+        copy.wait()
+
+    for n in range(2, len(smalls)):
+        small(n).start()
+
+    @pl.loop(0, steps)
+    def _(step):
+        attend(step)
 
     small(2).wait()
 
@@ -580,11 +575,8 @@
     bf16 = lambda *n: pltpu.VMEM(n, BF16)
     large = (queries, nk, nv, table, w, null, res)
     scratch = [pltpu.VMEM(value.shape, value.dtype) for value in large]
-    steps = heads // per_step
-    early = max(1, steps // 5)
-    for size in (early, early, steps - early, steps - early):
-        scratch.append(bf16(*keys.shape[:3], size * per_step * HEAD))
-    scratch += [dma(3, heads // per_step), dma(6)]
+    scratch += [bf16(*keys.shape), bf16(*keys.shape)]
+    scratch += [dma(3, keys.shape[0]), dma(6)]
     scratch += [
         f32(nc, picked, half), f32(8, vocab), f32(1, model_dim),
         bf16(model_dim, half), f32(model_dim, half), f32(2, 2, heads, half),

time: 91.6 us -> 88.5 us (0.966)
  Pallas kernels: 90.1 us -> 86.9 us
    pallas_call x1, Pallas kernels: 90.1 us -> 86.9 us  [run(): pl.pallas_call(functools.partial(kernel, places, per_step, min(4, nz)), i...]
where the time goes in v4:
time: 88.5 us; the launch traced here: 88.3 us
  Pallas kernels  86.9 us (98%)
  local copies, waits for them, and re-layouts  1.35 us (2%)
    pallas_call x1, Pallas kernels, run(): pl.pallas_call(functools.partial(kernel, places, per_step, min(4, nz)), i...  86.9 us

profile of v4, /device:TPU:33, one launch (start us, length us, event | category | flops | bytes accessed | tf_op | source)
XLA Modules:
  0.0 88.3 jit_solution(7701504329158057121)
XLA Ops:
  0.0 86.9 %rollout.1 = bf16[2,5120]{1,0:T(2,128)(2,1)} custom-call(s32[4]{0:T(128)} %refs_0_.1, s32[4]{0:T(128)} %refs_1_.1, s32[4,8]{1,0:T(4,128)} %refs_2_.1, bf16[256,5120]{1,0:T(8,128)(2,1)} %refs_3_.1, bf16[4,2,32,5120]{3,2,1,0:T(8,128)(2,1)} %refs_4_.1, bf16[4,2,32,5120]{3,2,1,0:T(8,128)(2,1)} %refs_5_.1, bf16[2,5120]{1,0:T(2,128)(2,1)} %refs_6_.1, ...), custom_call_target="tpu_custom_call" | custom-call | tf_op jit(solution)/shard_map/rollout/pallas_call | solution.py:599
  87.0 1.3 %copy.14 = bf16[2,5120]{1,0:T(2,128)(2,1)} copy(bf16[2,5120]{1,0:T(2,128)(2,1)} %rollout.1) | data formatting | bytes 40960

commit v5 on v4

--- a/solution.py
+++ b/solution.py
@@ -25,7 +25,7 @@
     (
         slot_ref, cached_ref, act_ref, q_in, k_in, v_in, nk_in, nv_in, table_in,
         w_in, null_in, res_in, out_ref,
-        q_ref, nk_ref, nv_ref, table_ref, w_ref, null_ref, res_ref, k_ref, v_ref, in_s, small_s,
+        q_ref, nk_ref, nv_ref, table_ref, w_ref, null_ref, res_ref, k_a, v_a, k_b, v_b, in_s, small_s,
         bias, count, gate, away, home, ml, mlp, scale, joint, mlx, ratio,
         ra, d, rel, relout, fin1, fin2, xs, zr, zms, zmr, fz, acc,
         wn, att, attg, wbuf, pr, prr, fin, finr,
@@ -60,6 +60,8 @@
     share = nz // nc
     width = per_step * HEAD
     steps = heads // per_step
+    early = k_a.shape[3] // width
+    spans = ((0, early, k_a, v_a), (early, steps, k_b, v_b))
     barrier = pltpu.get_barrier_semaphore()
 
     def near_id(j):
@@ -95,15 +97,6 @@
     def greet(where):
         pl.semaphore_signal(barrier, inc=1, device_id=where, device_id_type=MESH)
 
-    @pl.loop(1, nz)
-    def _(i):
-        greet({"z": far_peer(i)})
-
-    @pl.loop(1, near)
-    def _(i):
-        greet(twin_id(near_peer(i)))
-        greet(near_id(near_peer(i)))
-
     smalls = (
         (nk_in, nk_ref), (nv_in, nv_ref), (w_in, w_ref), (table_in, table_ref),
         (null_in, null_ref), (res_in, res_ref),
@@ -112,22 +105,28 @@
     def small(n):
         return pltpu.make_async_copy(*smalls[n], small_s.at[n])
 
-    def load(n):
-        band = rows // k_in.shape[0]
-        part = pl.ds(pl.multiple_of(n * band, band), band)
-        return (
-            pltpu.make_async_copy(k_in.at[n], k_ref.at[n], in_s.at[0, n]),
-            pltpu.make_async_copy(q_in.at[part], q_ref.at[part], in_s.at[1, n]),
-            pltpu.make_async_copy(v_in.at[n], v_ref.at[n], in_s.at[2, n]),
-        )
+    def load(which):
+        begin, end, k_to, v_to = spans[which]
+        part = slice(begin * width, end * width)
+        return [
+            pltpu.make_async_copy(k_in.at[:, :, :, part], k_to, in_s.at[0, which]),
+            pltpu.make_async_copy(q_in.at[:, part], q_ref.at[:, part], in_s.at[1, which]),
+            pltpu.make_async_copy(v_in.at[:, :, :, part], v_to, in_s.at[2, which]),
+        ]
 
     small(0).start()
     small(1).start()
-
-    @pl.loop(0, k_in.shape[0])
-    def _(n):
-        for copy in load(n):
-            copy.start()
+    for copy in load(0):
+        copy.start()
+
+    @pl.loop(1, nz)
+    def _(i):
+        greet({"z": far_peer(i)})
+
+    @pl.loop(1, near)
+    def _(i):
+        greet(twin_id(near_peer(i)))
+        greet(near_id(near_peer(i)))
 
     key = lax.broadcasted_iota(jnp.int32, (keys, half), 0)
     row = lax.broadcasted_iota(jnp.int32, (keys, half), 1)
@@ -174,19 +173,20 @@
     small(0).wait()
     small(1).wait()
 
-    def attend(step):
+    def attend(step, begin, k_ref, v_ref):
         work = []
         for i in range(per_step):
             head = step * per_step + i
             part = pl.ds(pl.multiple_of(head * HEAD, HEAD), HEAD)
+            into = pl.ds(pl.multiple_of((head - begin * per_step) * HEAD, HEAD), HEAD)
             few_keys = few(nk_ref, part)
             for which in (other, c):
                 q = q_ref[pl.ds(pl.multiple_of(which * half, half), half), part]
-                k = taken(k_ref, few_keys, part, which)
+                k = taken(k_ref, few_keys, into, which)
                 s = lax.dot_general(k, q, LAST, preferred_element_type=F32)
-                work.append((head, part, which, s))
+                work.append((head, part, into, which, s))
         ready = []
-        for head, part, which, s in work:
+        for head, part, into, which, s in work:
             s = s * factor + bias[which]
             top = jnp.max(s, 0, keepdims=True)
             p = jnp.exp2(s - top)
@@ -194,26 +194,41 @@
             first = 0 if which is other else 1
             ml[first, 0, pl.ds(head, 1), :] = top
             ml[first, 1, pl.ds(head, 1), :] = total
-            ready.append((part, which, p.astype(BF16)))
-        for part, which, p in ready:
-            v = taken(v_ref, few(nv_ref, part), part, which)
+            ready.append((part, into, which, p.astype(BF16)))
+        for part, into, which, p in ready:
+            v = taken(v_ref, few(nv_ref, part), into, which)
             numer = lax.dot_general(v, p, FIRST, preferred_element_type=F32)
             if which is other:
                 away[part, :] = numer.astype(BF16)
             else:
                 home[part, :] = numer
 
-    for copy in [copy for n in range(k_in.shape[0]) for copy in load(n)]:
+    def pass_on(begin, end):
+        @pl.loop(begin * width // wide, end * width // wide)
+        def _(t):
+            part = pl.ds(pl.multiple_of(t * wide, PIECE), wide)
+            send(away.at[part], ra.at[part], a_s, a_r.at[t], {"core": other})
+
+    for copy in load(0):
         copy.wait()
-
+    for copy in load(1):
+        copy.start()
+
+    @pl.loop(0, early)
+    def _(step):
+        attend(step, 0, k_a, v_a)
+
+    pl.semaphore_wait(barrier, nz + 2 * near - 3)
+    pass_on(0, early)
+    for copy in load(1):
+        copy.wait()
     for n in range(2, len(smalls)):
         small(n).start()
 
-    @pl.loop(0, steps)
+    @pl.loop(early, steps)
     def _(step):
-        attend(step)
-
-    small(2).wait()
+        attend(step, early, k_b, v_b)
+
 
     def turn(k):
         odd = lax.rem(k, 2)
@@ -242,8 +257,8 @@
             there = ra[r, :].astype(F32) * scale[1, pl.ds(h, 1), :]
             d[r, :] = (here + there).astype(BF16)
         ahead, behind = ways(t)
-        send(d.at[rows_of(t, opposite)], rel.at[t], o_s.at[t], o_r.at[t], {"x": ahead})
-        send(d.at[rows_of(t, behind)], fin2.at[t], d_s.at[t], d_r.at[t], {"x": behind})
+        send(d.at[rows_of(t, opposite)], rel.at[t], o_s, o_r.at[t], {"x": ahead})
+        send(d.at[rows_of(t, behind)], fin2.at[t], d_s, d_r.at[t], {"x": behind})
 
     def scaled(t, xx, n):
         g = t * (wide // PIECE) + xx * pieces + n
@@ -260,7 +275,7 @@
             r = slice(n * PIECE, (n + 1) * PIECE)
             value = value + rel[t, r, :].astype(F32) * ratio[behind, pl.ds(h, 1), :]
             relout[t, r, :] = value.astype(BF16)
-        send(relout.at[t], fin1.at[t], r_s.at[t], r_r.at[t], {"x": ahead})
+        send(relout.at[t], fin1.at[t], r_s, r_r.at[t], {"x": ahead})
 
     def settle(k):
         t = turn(k)
@@ -275,7 +290,7 @@
 
         @pl.when(k < nz - 1)
         def _():
-            send(xs.at[t], zr.at[z], z_s.at[t], z_r.at[z], {"z": t})
+            send(xs.at[t], zr.at[z], z_s, z_r.at[z], {"z": t})
 
     def wpart(j):
         return pl.ds(pl.multiple_of(j * cols, cols), cols)
@@ -283,16 +298,9 @@
     def wplace(zz, j):
         return zz * near + j
 
-    pl.semaphore_wait(barrier, nz + 2 * near - 3)
-
     send(ml.at[0], mlp, ml_s, ml_r, {"core": other})
-
-    @pl.loop(0, nz)
-    def _(k):
-        t = turn(k)
-        part = pl.ds(pl.multiple_of(t * wide, PIECE), wide)
-        send(away.at[part], ra.at[part], a_s.at[t], a_r.at[t], {"core": other})
-
+    pass_on(early, steps)
+    small(2).wait()
     send(w_ref, wn, wn_s, wn_r, {"z": twin})
 
     got(mlp, ml_r)
@@ -306,7 +314,7 @@
     @pl.loop(1, nx)
     def _(i):
         xx = lax.rem(x + i, nx)
-        send(joint, mlx.at[x], mx_s.at[xx], mx_r.at[x], {"x": xx})
+        send(joint, mlx.at[x], mx_s, mx_r, {"x": xx})
 
     mlx[x] = joint[...]
 
@@ -314,10 +322,7 @@
     def _(k):
         merge(k)
 
-    @pl.loop(1, nx)
-    def _(i):
-        xx = lax.rem(x + i, nx)
-        got(mlx.at[xx], mx_r.at[xx])
+    got(mlx.at[pl.ds(0, nx - 1)], mx_r)
 
     top = mlx[0, 0]
     for xx in range(1, nx):
@@ -344,7 +349,7 @@
     @pl.loop(1, nz)
     def _(i):
         t = far_peer(i)
-        send(zms.at[t], zmr.at[z], zm_s.at[t], zm_r.at[z], {"z": t})
+        send(zms.at[t], zmr.at[z], zm_s, zm_r, {"z": t})
 
     @pl.loop(lag, nz + 2 * lag)
     def _(k):
@@ -367,11 +372,11 @@
         j = near_peer(i)
         send(
             w_ref.at[:, wpart(j)], wbuf.at[wplace(parity, me)],
-            w_s.at[0, j], w_r.at[0, me], near_id(j),
+            w_s, w_r, near_id(j),
         )
         send(
             wn.at[:, wpart(j)], wbuf.at[wplace(1 - parity, me)],
-            w_s.at[1, j], w_r.at[1, me], near_id(j),
+            w_s, w_r, near_id(j),
         )
 
     wbuf[wplace(parity, me)] = w_ref[:, wpart(me)]
@@ -379,10 +384,7 @@
     zr[z] = xs[z]
     zmr[z] = zms[z]
 
-    @pl.loop(1, nz)
-    def _(i):
-        t = far_peer(i)
-        got(zmr.at[t], zm_r.at[t])
+    got(zmr.at[pl.ds(0, nz - 1)], zm_r)
 
     top = zmr[0, 0:2, :]
     for t in range(1, nz):
@@ -423,7 +425,7 @@
         @pl.when((goal != z) | (j != me))
         def _():
             send(
-                att, attg.at[spot_of], at_s.at[j], at_r.at[spot_of],
+                att, attg.at[spot_of], at_s, at_r,
                 {"z": goal, "x": j // nc, "core": lax.rem(j, nc)},
             )
 
@@ -431,17 +433,15 @@
     def _():
         attg[spot_of] = att[...]
 
-    @pl.loop(1, near)
-    def _(i):
-        j = near_peer(i)
-        got(wbuf.at[wplace(parity, j)], w_r.at[0, j])
-        got(wbuf.at[wplace(1 - parity, j)], w_r.at[1, j])
-
-    @pl.loop(0, near)
-    def _(i):
-        @pl.when((goal != z) | (i != spot_of))
-        def _():
-            got(attg.at[i], at_r.at[i])
+    got(wbuf.at[pl.ds(0, 2 * near - 2)], w_r)
+
+    @pl.when(goal == z)
+    def _():
+        got(attg.at[pl.ds(0, near - 1)], at_r)
+
+    @pl.when(goal != z)
+    def _():
+        got(attg, at_r)
 
     product = None
     for i in range(near):
@@ -465,7 +465,7 @@
 
         @pl.when(t != z)
         def _():
-            send(pr.at[n], prr.at[z // nc], p_s.at[n], p_r.at[z // nc], {"z": t})
+            send(pr.at[n], prr.at[z // nc], p_s, p_r, {"z": t})
 
     @pl.when(z // share == parity)
     def _():
@@ -481,11 +481,14 @@
         sums = jnp.dot(count[...].astype(BF16), table_ref[:, spread], preferred_element_type=F32)
         gate[:, spread] = 1.0 + sums[0:1, :] / acts
 
-    @pl.loop(0, share)
-    def _(i):
-        @pl.when(i * nc + z // share != z)
-        def _():
-            got(prr.at[i], p_r.at[i])
+    @pl.when(z // share == parity)
+    def _():
+        if share > 1:
+            got(prr.at[pl.ds(0, share - 1)], p_r)
+
+    @pl.when(z // share != parity)
+    def _():
+        got(prr, p_r)
 
     sums = prr[0].astype(F32)
     for t in range(1, share):
@@ -496,14 +499,11 @@
     @pl.loop(1, near)
     def _(i):
         j = near_peer(i)
-        send(fin.at[j], finr.at[me], f_s.at[j], f_r.at[me], near_id(j))
+        send(fin.at[j], finr.at[me], f_s, f_r, near_id(j))
 
     finr[me] = fin[me]
 
-    @pl.loop(1, near)
-    def _(i):
-        j = near_peer(i)
-        got(finr.at[j], f_r.at[j])
+    got(finr.at[pl.ds(0, near - 1)], f_r)
 
     even = (lax.broadcasted_iota(jnp.int32, (own, cols), 0) & 1) == 0
     for j in range(near):
@@ -514,41 +514,32 @@
     gone(mlp, ml_s)
     gone(wn, wn_s)
 
-    @pl.loop(1, nx)
-    def _(i):
-        gone(joint, mx_s.at[lax.rem(x + i, nx)])
-
-    @pl.loop(1, near)
-    def _(i):
-        j = near_peer(i)
-        gone(wbuf.at[0], w_s.at[0, j])
-        gone(wbuf.at[0], w_s.at[1, j])
-        gone(fin.at[0], f_s.at[j])
-
-    @pl.loop(0, near)
-    def _(j):
-        @pl.when((goal != z) | (j != me))
-        def _():
-            gone(att, at_s.at[j])
-
-    @pl.loop(0, share)
-    def _(n):
-        @pl.when(parity * share + n != z)
-        def _():
-            gone(pr.at[0], p_s.at[n])
-
-    @pl.loop(0, nz)
-    def _(t):
-        gone(ra.at[pl.ds(0, wide)], a_s.at[t])
-        gone(rel.at[0], o_s.at[t])
-        gone(fin2.at[0], d_s.at[t])
-        gone(relout.at[0], r_s.at[t])
-
-    @pl.loop(1, nz)
-    def _(i):
-        t = far_peer(i)
-        gone(zms.at[0], zm_s.at[t])
-        gone(xs.at[0], z_s.at[t])
+    gone(mlx.at[pl.ds(0, nx - 1)], mx_s)
+    gone(wbuf.at[pl.ds(0, 2 * near - 2)], w_s)
+    gone(fin.at[pl.ds(0, near - 1)], f_s)
+    gone(ra, a_s)
+    gone(rel, o_s)
+    gone(fin2, d_s)
+    gone(relout, r_s)
+    gone(zms.at[pl.ds(0, nz - 1)], zm_s)
+    gone(xs.at[pl.ds(0, nz - 1)], z_s)
+
+    @pl.when(goal == z)
+    def _():
+        gone(attg.at[pl.ds(0, near - 1)], at_s)
+
+    @pl.when(goal != z)
+    def _():
+        gone(attg, at_s)
+
+    @pl.when(z // share == parity)
+    def _():
+        if share > 1:
+            gone(pr.at[pl.ds(0, share - 1)], p_s)
+
+    @pl.when(z // share != parity)
+    def _():
+        gone(pr, p_s)
 
 
 def run(places, slot_of, cached, actions, queries, keys, values, nk, nv, table, w, null, res):
@@ -575,8 +566,10 @@
     bf16 = lambda *n: pltpu.VMEM(n, BF16)
     large = (queries, nk, nv, table, w, null, res)
     scratch = [pltpu.VMEM(value.shape, value.dtype) for value in large]
-    scratch += [bf16(*keys.shape), bf16(*keys.shape)]
-    scratch += [dma(3, keys.shape[0]), dma(6)]
+    early = nz // 2 * wide
+    for size in (early, early, model_dim - early, model_dim - early):
+        scratch.append(bf16(*keys.shape[:3], size))
+    scratch += [dma(3, 2), dma(6)]
     scratch += [
         f32(nc, picked, half), f32(8, vocab), f32(1, model_dim),
         bf16(model_dim, half), f32(model_dim, half), f32(2, 2, heads, half),
@@ -590,12 +583,10 @@
         bf16(share, half // share, cols), bf16(share, half // share, cols),
         f32(near, own, cols), f32(near, own, cols),
     ]
-    scratch += [pltpu.SemaphoreType.DMA, pltpu.SemaphoreType.DMA]
-    for size in (nx, nz, nz, nz, nz, nz, nz):
-        scratch += [dma(size), dma(size)]
-    scratch += [pltpu.SemaphoreType.DMA, pltpu.SemaphoreType.DMA]
-    scratch += [dma(near), dma(near), dma(2, near), dma(2, near)]
-    scratch += [dma(share), dma(share), dma(near), dma(near)]
+    one = pltpu.SemaphoreType.DMA
+    scratch += [one] * 4
+    scratch += [one, dma(nz)] * 5
+    scratch += [one] * 12
     return pl.pallas_call(
         functools.partial(kernel, places, per_step, min(4, nz)),
         in_specs=[smem] * 3 + [away] * 9,

time: 88.5 us -> 84.3 us (0.953)
  Pallas kernels: 86.9 us -> 82.7 us
    pallas_call x1, Pallas kernels: 86.9 us -> 82.7 us  [run(): pl.pallas_call(functools.partial(kernel, places, per_step, min(4, nz)), i...]
where the time goes in v5:
time: 84.3 us; the launch traced here: 84.1 us
  Pallas kernels  82.7 us (98%)
  local copies, waits for them, and re-layouts  1.35 us (2%)
    pallas_call x1, Pallas kernels, run(): pl.pallas_call(functools.partial(kernel, places, per_step, min(4, nz)), i...  82.7 us

profile of v5, /device:TPU:33, one launch (start us, length us, event | category | flops | bytes accessed | tf_op | source)
XLA Modules:
  0.0 84.1 jit_solution(3082382115462184303)
XLA Ops:
  0.0 82.7 %rollout.1 = bf16[2,5120]{1,0:T(2,128)(2,1)} custom-call(s32[4]{0:T(128)} %refs_0_.1, s32[4]{0:T(128)} %refs_1_.1, s32[4,8]{1,0:T(4,128)} %refs_2_.1, bf16[256,5120]{1,0:T(8,128)(2,1)} %refs_3_.1, bf16[4,2,32,5120]{3,2,1,0:T(8,128)(2,1)} %refs_4_.1, bf16[4,2,32,5120]{3,2,1,0:T(8,128)(2,1)} %refs_5_.1, bf16[2,5120]{1,0:T(2,128)(2,1)} %refs_6_.1, ...), custom_call_target="tpu_custom_call" | custom-call | tf_op jit(solution)/shard_map/rollout/pallas_call | solution.py:590
  82.8 1.3 %copy.14 = bf16[2,5120]{1,0:T(2,128)(2,1)} copy(bf16[2,5120]{1,0:T(2,128)(2,1)} %rollout.1) | data formatting | bytes 40960

commit v6 on v5

--- a/solution.py
+++ b/solution.py
@@ -114,10 +114,17 @@
             pltpu.make_async_copy(v_in.at[:, :, :, part], v_to, in_s.at[2, which]),
         ]
 
+    def wpart(j):
+        return pl.ds(pl.multiple_of(j * cols, cols), cols)
+
+    def wplace(zz, j):
+        return zz * near + j
+
     small(0).start()
     small(1).start()
     for copy in load(0):
         copy.start()
+    small(2).start()
 
     @pl.loop(1, nz)
     def _(i):
@@ -220,9 +227,17 @@
 
     pl.semaphore_wait(barrier, nz + 2 * near - 3)
     pass_on(0, early)
+    small(2).wait()
+    send(w_ref, wn, wn_s, wn_r, {"z": twin})
+
+    @pl.loop(1, near)
+    def _(i):
+        j = near_peer(i)
+        send(w_ref.at[:, wpart(j)], wbuf.at[wplace(parity, me)], w_s, w_r, near_id(j))
+
     for copy in load(1):
         copy.wait()
-    for n in range(2, len(smalls)):
+    for n in range(3, len(smalls)):
         small(n).start()
 
     @pl.loop(early, steps)
@@ -292,16 +307,8 @@
         def _():
             send(xs.at[t], zr.at[z], z_s, z_r.at[z], {"z": t})
 
-    def wpart(j):
-        return pl.ds(pl.multiple_of(j * cols, cols), cols)
-
-    def wplace(zz, j):
-        return zz * near + j
-
     send(ml.at[0], mlp, ml_s, ml_r, {"core": other})
     pass_on(early, steps)
-    small(2).wait()
-    send(w_ref, wn, wn_s, wn_r, {"z": twin})
 
     got(mlp, ml_r)
     top = jnp.maximum(ml[1, 0], mlp[0])
@@ -370,10 +377,6 @@
     @pl.loop(1, near)
     def _(i):
         j = near_peer(i)
-        send(
-            w_ref.at[:, wpart(j)], wbuf.at[wplace(parity, me)],
-            w_s, w_r, near_id(j),
-        )
         send(
             wn.at[:, wpart(j)], wbuf.at[wplace(1 - parity, me)],
             w_s, w_r, near_id(j),

time: 84.3 us -> 81.7 us (0.969)
  Pallas kernels: 82.7 us -> 80.1 us
    pallas_call x1, Pallas kernels: 82.7 us -> 80.1 us  [run(): pl.pallas_call(functools.partial(kernel, places, per_step, min(4, nz)), i...]
where the time goes in v6:
time: 81.7 us; the launch traced here: 81.5 us
  Pallas kernels  80.1 us (98%)
  local copies, waits for them, and re-layouts  1.35 us (2%)
    pallas_call x1, Pallas kernels, run(): pl.pallas_call(functools.partial(kernel, places, per_step, min(4, nz)), i...  80.1 us

profile of v6, /device:TPU:33, one launch (start us, length us, event | category | flops | bytes accessed | tf_op | source)
XLA Modules:
  0.0 81.5 jit_solution(8058715719638406917)
XLA Ops:
  0.0 80.1 %rollout.1 = bf16[2,5120]{1,0:T(2,128)(2,1)} custom-call(s32[4]{0:T(128)} %refs_0_.1, s32[4]{0:T(128)} %refs_1_.1, s32[4,8]{1,0:T(4,128)} %refs_2_.1, bf16[256,5120]{1,0:T(8,128)(2,1)} %refs_3_.1, bf16[4,2,32,5120]{3,2,1,0:T(8,128)(2,1)} %refs_4_.1, bf16[4,2,32,5120]{3,2,1,0:T(8,128)(2,1)} %refs_5_.1, bf16[2,5120]{1,0:T(2,128)(2,1)} %refs_6_.1, ...), custom_call_target="tpu_custom_call" | custom-call | tf_op jit(solution)/shard_map/rollout/pallas_call | solution.py:593
  80.1 1.3 %copy.14 = bf16[2,5120]{1,0:T(2,128)(2,1)} copy(bf16[2,5120]{1,0:T(2,128)(2,1)} %rollout.1) | data formatting | bytes 40960

commit v7 on v6

--- a/solution.py
+++ b/solution.py
@@ -351,12 +351,22 @@
         zms[t, 1:2, :] = scale2[0, pl.ds(high, 1), :]
         zms[t, 2:3, :] = scale2[1, pl.ds(low, 1), :]
         zms[t, 3:4, :] = scale2[1, pl.ds(high, 1), :]
-        zms[t, 4:8, :] = jnp.zeros((4, half), F32)
 
     @pl.loop(1, nz)
     def _(i):
         t = far_peer(i)
         send(zms.at[t], zmr.at[z], zm_s, zm_r, {"z": t})
+
+    def twin_columns():
+        got(wn, wn_r)
+
+        @pl.loop(1, near)
+        def _(i):
+            j = near_peer(i)
+            send(
+                wn.at[:, wpart(j)], wbuf.at[wplace(1 - parity, me)],
+                w_s, w_r, near_id(j),
+            )
 
     @pl.loop(lag, nz + 2 * lag)
     def _(k):
@@ -368,19 +378,13 @@
         def _():
             relay(k - lag)
 
+        @pl.when(k == nz + lag - 1)
+        def _():
+            twin_columns()
+
         @pl.when(k >= 2 * lag)
         def _():
             settle(k - 2 * lag)
-
-    got(wn, wn_r)
-
-    @pl.loop(1, near)
-    def _(i):
-        j = near_peer(i)
-        send(
-            wn.at[:, wpart(j)], wbuf.at[wplace(1 - parity, me)],
-            w_s, w_r, near_id(j),
-        )
 
     wbuf[wplace(parity, me)] = w_ref[:, wpart(me)]
     wbuf[wplace(1 - parity, me)] = wn[:, wpart(me)]
@@ -580,7 +584,7 @@
         f32(nx, 2, heads, half), f32(nx, heads, half),
         bf16(model_dim, half), bf16(model_dim, half),
         *[bf16(nz, blk, half) for _ in range(6)],
-        f32(nz, 8, half), f32(nz, 8, half), f32(nz, 8, half), f32(blk, half),
+        f32(nz, 4, half), f32(nz, 4, half), f32(nz, 8, half), f32(blk, half),
         bf16(wrows, model_dim), bf16(nc, wrows, half), bf16(near, nc, wrows, half),
         bf16(2 * near, wrows, cols),
         bf16(share, half // share, cols), bf16(share, half // share, cols),

time: 81.7 us -> 81.5 us (level)
  no operation moved by 1% of the time
where the time goes in v7:
time: 81.5 us; the launch traced here: 81.3 us
  Pallas kernels  79.9 us (98%)
  local copies, waits for them, and re-layouts  1.35 us (2%)
    pallas_call x1, Pallas kernels, run(): pl.pallas_call(functools.partial(kernel, places, per_step, min(4, nz)), i...  79.9 us

profile of v7, /device:TPU:33, one launch (start us, length us, event | category | flops | bytes accessed | tf_op | source)
XLA Modules:
  0.0 81.3 jit_solution(6207911969462670718)
XLA Ops:
  0.0 79.9 %rollout.1 = bf16[2,5120]{1,0:T(2,128)(2,1)} custom-call(s32[4]{0:T(128)} %refs_0_.1, s32[4]{0:T(128)} %refs_1_.1, s32[4,8]{1,0:T(4,128)} %refs_2_.1, bf16[256,5120]{1,0:T(8,128)(2,1)} %refs_3_.1, bf16[4,2,32,5120]{3,2,1,0:T(8,128)(2,1)} %refs_4_.1, bf16[4,2,32,5120]{3,2,1,0:T(8,128)(2,1)} %refs_5_.1, bf16[2,5120]{1,0:T(2,128)(2,1)} %refs_6_.1, ...), custom_call_target="tpu_custom_call" | custom-call | tf_op jit(solution)/shard_map/rollout/pallas_call | solution.py:597
  79.9 1.3 %copy.14 = bf16[2,5120]{1,0:T(2,128)(2,1)} copy(bf16[2,5120]{1,0:T(2,128)(2,1)} %rollout.1) | data formatting | bytes 40960

commit v8 on v7

--- a/solution.py
+++ b/solution.py
@@ -595,7 +595,7 @@
     scratch += [one, dma(nz)] * 5
     scratch += [one] * 12
     return pl.pallas_call(
-        functools.partial(kernel, places, per_step, min(4, nz)),
+        functools.partial(kernel, places, per_step, min(3, nz)),
         in_specs=[smem] * 3 + [away] * 9,
         out_specs=vmem,
         out_shape=jax.ShapeDtypeStruct(res.shape, BF16),

time: 81.5 us -> 81.4 us (level)
  no operation moved by 1% of the time
where the time goes in v8:
time: 81.4 us; the launch traced here: 81.2 us
  Pallas kernels  79.9 us (98%)
  local copies, waits for them, and re-layouts  1.35 us (2%)
    pallas_call x1, Pallas kernels, run(): pl.pallas_call(functools.partial(kernel, places, per_step, min(3, nz)), i...  79.9 us

profile of v8, /device:TPU:33, one launch (start us, length us, event | category | flops | bytes accessed | tf_op | source)
XLA Modules:
  0.0 81.2 jit_solution(16217590362242694783)
XLA Ops:
  0.0 79.9 %rollout.1 = bf16[2,5120]{1,0:T(2,128)(2,1)} custom-call(s32[4]{0:T(128)} %refs_0_.1, s32[4]{0:T(128)} %refs_1_.1, s32[4,8]{1,0:T(4,128)} %refs_2_.1, bf16[256,5120]{1,0:T(8,128)(2,1)} %refs_3_.1, bf16[4,2,32,5120]{3,2,1,0:T(8,128)(2,1)} %refs_4_.1, bf16[4,2,32,5120]{3,2,1,0:T(8,128)(2,1)} %refs_5_.1, bf16[2,5120]{1,0:T(2,128)(2,1)} %refs_6_.1, ...), custom_call_target="tpu_custom_call" | custom-call | tf_op jit(solution)/shard_map/rollout/pallas_call | solution.py:597
  79.9 1.3 %copy.14 = bf16[2,5120]{1,0:T(2,128)(2,1)} copy(bf16[2,5120]{1,0:T(2,128)(2,1)} %rollout.1) | data formatting | bytes 40960
